TPU v7x, 8 devices: a whole 2x2x1 slice. The times are simulated.
8 devices in a mesh: dp: 4 (over z, y, x), pp: 2 (over core).
Axes of the slice: x: 2, y: 2, z: 1, core: 2. Of those that a mesh axis runs over, the one named last changes fastest.
Arguments:
- tok_ids: int32 [2, 8, 130], P(None, 'dp')
- emb_s: bfloat16 [2, 92544, 2048], P('pp', 'dp')
- w_one: bfloat16 [2, 2, 2048, 8192], P('pp')
- w_two: bfloat16 [2, 2, 8192, 2048], P('pp')
- gain_f: bfloat16 [2048], replicated
- gain_h: bfloat16 [2048], replicated
- gain_e: bfloat16 [2048], replicated
- gain_m: bfloat16 [2048], replicated
- w_proj: bfloat16 [4096, 2048], replicated
- u_one: bfloat16 [2048, 8192], replicated
- u_two: bfloat16 [8192, 2048], replicated
- w_out: bfloat16 [2048, 92544], replicated
Outputs:
- output 1: float32 [], replicated
- output 2: float32 [2, 8, 128], P(None, 'dp')
- output 3: float32 [2, 8, 128], P(None, 'dp')
All inputs are finite; a program needn't handle non-finite values.
Results may differ from a plain program's by a relative error of at most 0.00260037.
Values are sent between devices in bfloat16 or wider.
A program may use at most 2.75 GiB of HBM per device.

v0:
```python
import jax
import jax.numpy as jnp
from jax import lax
from jax.sharding import PartitionSpec as P

NORM_EPS = 1e-6
MTP_WEIGHT = 0.3
HEAD_ROWS = 128


def norm_plain(x_val):
    x_f = x_val.astype(jnp.float32)
    return (x_f * lax.rsqrt(jnp.mean(x_f * x_f, axis=-1, keepdims=True) + NORM_EPS)).astype(jnp.bfloat16)


def norm_gain(x_val, gain_vec):
    x_f = x_val.astype(jnp.float32)
    scaled = x_f * lax.rsqrt(jnp.mean(x_f * x_f, axis=-1, keepdims=True) + NORM_EPS)
    return (scaled * gain_vec.astype(jnp.float32)).astype(jnp.bfloat16)


def mlp_add(x_val, normed, w_up, w_down):
    hidden = jax.nn.gelu(jnp.dot(normed, w_up, preferred_element_type=jnp.float32)).astype(jnp.bfloat16)
    return (x_val.astype(jnp.float32) + jnp.dot(hidden, w_down, preferred_element_type=jnp.float32)).astype(jnp.bfloat16)


def mtp_depth(h_last, e_rows, gain_h, gain_e, gain_m, w_proj, u_one, u_two):
    row_width = h_last.shape[-1]
    z_sum = jnp.dot(norm_gain(h_last, gain_h), w_proj[:row_width], preferred_element_type=jnp.float32)
    z_sum = z_sum + jnp.dot(norm_gain(e_rows, gain_e), w_proj[row_width:], preferred_element_type=jnp.float32)
    z_val = z_sum.astype(jnp.bfloat16)
    return mlp_add(z_val, norm_gain(z_val, gain_m), u_one, u_two)


def token_nll(normed, targets, w_out):
    n_rows, row_width = normed.shape
    n_blocks = n_rows // HEAD_ROWS

    def one_block(pair):
        block_rows, block_tgt = pair
        logits = jnp.dot(block_rows, w_out, preferred_element_type=jnp.float32)
        picked = jnp.take_along_axis(logits, block_tgt[:, None], axis=1)[:, 0]
        return jax.nn.logsumexp(logits, axis=1) - picked

    per_block = lax.map(one_block, (normed.reshape(n_blocks, HEAD_ROWS, row_width), targets.reshape(n_blocks, HEAD_ROWS)))
    return per_block.reshape(n_rows)


def solution(mesh):
    n_stages = mesh.shape['pp']
    n_data = mesh.shape['dp']
    fwd_perm = [(stage_idx, stage_idx + 1) for stage_idx in range(n_stages - 1)]
    mtp_perm = [(0, n_stages - 1)]

    def body(tok_ids, emb_s, w_one, w_two, gain_f, gain_h, gain_e, gain_m, w_proj, u_one, u_two, w_out):
        stage = lax.axis_index('pp')
        n_micro, batch_dev, seq_plus = tok_ids.shape
        seq_len = seq_plus - 2
        n_layers = w_one.shape[1]
        row_width = w_one.shape[2]
        n_rows = batch_dev * seq_len
        is_first = stage == 0
        is_last = stage == n_stages - 1
        table = lax.all_gather(emb_s[0], 'dp', axis=0, tiled=True)

        def head_losses(h_last, e_rows, ids_out):
            main_nll = token_nll(norm_gain(h_last, gain_f), ids_out[:, 1:seq_len + 1].reshape(n_rows), w_out)
            z_val = mtp_depth(h_last, e_rows, gain_h, gain_e, gain_m, w_proj, u_one, u_two)
            mtp_nll = token_nll(norm_gain(z_val, gain_f), ids_out[:, 2:].reshape(n_rows), w_out)
            return main_nll, mtp_nll

        def no_losses(h_last, e_rows, ids_out):
            zero_rows = jnp.zeros((n_rows,), jnp.float32)
            return zero_rows, zero_rows

        def tick_step(state, t_idx):
            ids_in = lax.dynamic_index_in_dim(tok_ids, jnp.minimum(t_idx, n_micro - 1), axis=0, keepdims=False)
            out_idx = jnp.maximum(t_idx - (n_stages - 1), 0)
            ids_out = lax.dynamic_index_in_dim(tok_ids, out_idx, axis=0, keepdims=False)
            x_val = jnp.where(is_first, table[ids_in[:, :seq_len].reshape(n_rows)], state)
            for layer in range(n_layers):
                x_val = mlp_add(x_val, norm_plain(x_val), w_one[0, layer], w_two[0, layer])
            e_rows = lax.ppermute(table[ids_out[:, 1:seq_len + 1].reshape(n_rows)], 'pp', mtp_perm)
            losses = lax.cond(is_last & (t_idx >= n_stages - 1), head_losses, no_losses, x_val, e_rows, ids_out)
            return lax.ppermute(x_val, 'pp', fwd_perm), losses

        init_state = jnp.zeros((n_rows, row_width), jnp.bfloat16)
        _, (main_all, mtp_all) = lax.scan(tick_step, init_state, jnp.arange(n_micro + n_stages - 1))
        main_nll = lax.psum(main_all[n_stages - 1:], 'pp').reshape(n_micro, batch_dev, seq_len)
        mtp_nll = lax.psum(mtp_all[n_stages - 1:], 'pp').reshape(n_micro, batch_dev, seq_len)
        local_sum = jnp.sum(main_nll) + MTP_WEIGHT * jnp.sum(mtp_nll)
        total_loss = lax.psum(local_sum, 'dp') / (n_micro * batch_dev * n_data * seq_len)
        return total_loss, main_nll, mtp_nll

    replicated = P()
    in_specs = (P(None, 'dp', None), P('pp', 'dp', None), P('pp'), P('pp'), replicated, replicated, replicated, replicated, replicated, replicated, replicated, replicated)
    out_specs = (replicated, P(None, 'dp', None), P(None, 'dp', None))
    return jax.shard_map(body, mesh=mesh, in_specs=in_specs, out_specs=out_specs, check_vma=False)
```

profile of v0, /device:TPU:0, one launch (start us, length us, event | category | flops | bytes accessed | tf_op | source)
XLA Modules:
  0.0 4813.8 jit_solution(13574258969993902602)
XLA Ops:
  7.2 0.7 all-gather.3.cloned.1.call-update
  8.0 3174.4 %all-gather.3.cloned.1.call-done = bf16[1,92544,2048]{2,1,0:T(8,128)(2,1)} async-done(((bf16[1,23136,2048]{2,1,0:T(8,128)(2,1)}), bf16[1,92544,2048]{2,1,0:T(8,128)(2,1)}) %all-gather.3.cloned.1.call-update) | async-done | bytes 379060224 | tf_op jit(solution)/shard_map/all_gather | solution.py:64
  3182.9 1.1 broadcast_in_dim.46
  3184.0 949.1 %while.36 = (s32[]{:T(128)}, bf16[256,2048]{1,0:T(8,128)(2,1)}, f32[3,256]{1,0:T(4,128)}, f32[3,256]{1,0:T(4,128)}, pred[]{:T(512)}, /*index=5*/s32[3]{0:T(128)}...) while((s32[]{:T(128)}, bf16[256,2048]{1,0:T(8,128)(2,1)}, ...), condition=%wide.region_17.19_spmd, body=%wide.region_0.18_spmd.sunk | while | flops 153032097792 | bytes 1289686272 | solution.py:88
  3207.8 1.2 dynamic_slice.69
  3210.3 0.8 dynamic-slice_bitcast_fusion.3
  3211.7 4.0 gather_fusion.3
  3215.7 1.6 collective-permute-start.1
  3217.3 4.0 gather_fusion.2
  3221.8 28.0 fusion.211
  3249.8 18.3 fusion.108.clone.11
  3268.2 17.1 fusion.212
  3285.2 8.5 collective-permute-start
  3294.4 1.1 conditional.2
  3295.6 1.3 dynamic_update_slice.24
  3296.9 1.3 dynamic_update_slice.25
  3298.2 1.2 dynamic_slice.69
  3300.7 0.7 dynamic-slice_bitcast_fusion.3
  3301.9 4.0 gather_fusion.3
  3306.0 1.4 collective-permute-start.1
  3307.4 4.0 gather_fusion.2
  3311.9 28.0 fusion.211
  3339.9 18.3 fusion.108.clone.11
  3358.3 17.1 fusion.212
  3375.3 7.5 collective-permute-start
  3383.6 1.1 conditional.2
  3384.7 1.3 dynamic_update_slice.24
  3386.0 1.3 dynamic_update_slice.25
  3387.3 1.2 dynamic_slice.69
  3389.8 0.8 dynamic-slice_bitcast_fusion.3
  3391.1 4.0 gather_fusion.3
  3395.2 657.0 %collective-permute-start.1 = (bf16[256,2048]{1,0:T(8,128)(2,1)S(1)}, bf16[256,2048]{1,0:T(8,128)(2,1)S(1)}, u32[]{:S(2)}, u32[]{:S(2)}) collective-permute-start(bf16[256,2048]{1,0:T(8,128)(2,1)S(1)} %gather_fusion.3), channel_id=1, source_target_pairs={{0,1},{2,3},{4,5},{6,7}} | collective-permute-start | bytes 3145736 | tf_op jit(solution)/shard_map/while/body/eval_jaxpr/ppermute | solution.py:83
  4052.2 4.0 gather_fusion.2
  4056.7 28.0 fusion.211
  4084.7 18.3 fusion.108.clone.11
  4103.1 17.1 fusion.212
  4120.2 8.5 collective-permute-start
  4129.4 1.1 conditional.2
  4130.5 1.3 dynamic_update_slice.24
  4131.8 1.3 dynamic_update_slice.25
  4133.1 0.7 slice.54
  4133.8 0.7 slice.55
  4134.5 657.1 %all-reduce = (f32[2,256]{1,0:T(2,128)S(1)}, f32[2,256]{1,0:T(2,128)S(1)}) all-reduce(f32[2,256]{1,0:T(2,128)S(1)} %slice.54, f32[2,256]{1,0:T(2,128)S(1)} %slice.55), channel_id=1, replica_groups=mesh['dp'=4,'pp'=2] {'pp'}, use_global_device_ids=true, to_apply=%region_18.20 | all-reduce | flops 1024 | bytes 8192 | tf_op jit(solution)/shard_map/psum | solution.py:89
  4791.6 0.6 reshape.256
  4792.2 0.6 reduce_sum.100
  4792.8 0.6 reduce_sum.101
  4794.7 0.6 reshape.257
  4795.3 9.5 psum.23
  (73 shorter events, 7.1 us)
Async XLA Ops:
  7.2 3176.8 %copy-start.5 = (bf16[2048]{0:T(1024)(128)(2,1)S(1)}, bf16[2048]{0:T(1024)(128)(2,1)}, u32[]{:S(2)}) copy-start(bf16[2048]{0:T(1024)(128)(2,1)} %param.27) | copy-start | bytes 12292
  7.2 3176.8 %copy-start.6 = (bf16[2048]{0:T(1024)(128)(2,1)S(1)}, bf16[2048]{0:T(1024)(128)(2,1)}, u32[]{:S(2)}) copy-start(bf16[2048]{0:T(1024)(128)(2,1)} %param.28) | copy-start | bytes 12292
  7.2 3176.8 %copy-start.7 = (bf16[2048]{0:T(1024)(128)(2,1)S(1)}, bf16[2048]{0:T(1024)(128)(2,1)}, u32[]{:S(2)}) copy-start(bf16[2048]{0:T(1024)(128)(2,1)} %param.29) | copy-start | bytes 12292
  7.2 3175.1 %all-gather.3.cloned.1.call-start = ((), (), s32[]{:S(2)}) async-start(), calls=%async_computation | async-start | bytes 473825280 | tf_op jit(solution)/shard_map/all_gather | solution.py:64
  3211.1 0.6 copy-start.1
  3215.7 78.7 %collective-permute-start.1 = (bf16[256,2048]{1,0:T(8,128)(2,1)S(1)}, bf16[256,2048]{1,0:T(8,128)(2,1)S(1)}, u32[]{:S(2)}, u32[]{:S(2)}) collective-permute-start(bf16[256,2048]{1,0:T(8,128)(2,1)S(1)} %gather_fusion.3), channel_id=1, source_target_pairs={{0,1},{2,3},{4,5},{6,7}} | collective-permute-start | bytes 3145736 | tf_op jit(solution)/shard_map/while/body/eval_jaxpr/ppermute | solution.py:83
  3249.8 18.3 copy-start.9
  3268.2 26.3 copy-start.2
  3268.2 26.3 copy-start.4
  3285.2 12.9 collective-permute-start
  3301.4 0.6 copy-start.1
  3306.0 77.5 %collective-permute-start.1 = (bf16[256,2048]{1,0:T(8,128)(2,1)S(1)}, bf16[256,2048]{1,0:T(8,128)(2,1)S(1)}, u32[]{:S(2)}, u32[]{:S(2)}) collective-permute-start(bf16[256,2048]{1,0:T(8,128)(2,1)S(1)} %gather_fusion.3), channel_id=1, source_target_pairs={{0,1},{2,3},{4,5},{6,7}} | collective-permute-start | bytes 3145736 | tf_op jit(solution)/shard_map/while/body/eval_jaxpr/ppermute | solution.py:83
  3339.9 18.3 copy-start.9
  3358.2 25.3 copy-start.2
  3358.3 25.3 copy-start.4
  3375.3 11.9 collective-permute-start
  3390.5 0.6 copy-start.1
  3395.2 734.2 %collective-permute-start.1 = (bf16[256,2048]{1,0:T(8,128)(2,1)S(1)}, bf16[256,2048]{1,0:T(8,128)(2,1)S(1)}, u32[]{:S(2)}, u32[]{:S(2)}) collective-permute-start(bf16[256,2048]{1,0:T(8,128)(2,1)S(1)} %gather_fusion.3), channel_id=1, source_target_pairs={{0,1},{2,3},{4,5},{6,7}} | collective-permute-start | bytes 3145736 | tf_op jit(solution)/shard_map/while/body/eval_jaxpr/ppermute | solution.py:83
  4084.7 18.3 copy-start.9
  4103.1 26.3 copy-start.2
  4103.1 26.3 copy-start.4
  4120.2 12.9 collective-permute-start
Sparse Core Ops, SparseCore 0:
  9.8 3172.4 all-gather.2
where the time goes:
time: 4820 us; the launch traced here: 4810 us
  waiting for transfers between devices  3180 us (66%)
  starting transfers between devices  684 us (14%)
  blocking collectives  667 us (14%)
  matrix products  190 us (4%)
    all_gather x1, waiting for transfers between devices, body(): table = lax.all_gather(emb_s[0], 'dp', axis=0, tiled=True)  3170 us
    ppermute x3, starting transfers between devices, tick_step(): lax.ppermute(table[ids_out[:, 1:seq_len + 1].reshape(n_rows)], 'pp', mtp_...  660 us
    psum x1, blocking collectives, body(): lax.psum(main_all[n_stages - 1:], 'pp').reshape(n_micro, batch_dev, seq_len)  657 us
    dot_general x6, matrix products, mlp_add(): jnp.dot(hidden, w_down, preferred_element_type=jnp.float32)  135 us
  transfers between devices with their start and end apart: 7, of which 1 were waited for; matrix products, arithmetic and copies ran while one was open for 4% of the time, Pallas kernels for 0%

commit v1 on v0

v1 whole, which is shorter than its diff:
```python
import functools

import jax
import jax.numpy as jnp
from jax import lax
from jax.experimental import pallas as pl
from jax.experimental.pallas import tpu as pltpu
from jax.sharding import PartitionSpec as P

NORM_EPS = 1e-6
MTP_WEIGHT = 0.3
F32 = jnp.float32
BF16 = jnp.bfloat16
VMEM_BYTES = 60 * 1024 * 1024

ROWS_A = 288
FFN_TILE = 1024
HEAD_HALF = 1024
CAP_A = 104
CAP_B = 88


def rms(x_f):
    return x_f * lax.rsqrt(jnp.mean(x_f * x_f, axis=-1, keepdims=True) + NORM_EPS)


def rms_gain(x_val, gain_ref):
    return (rms(x_val.astype(F32)) * gain_ref[...].astype(F32)).astype(BF16)


def dot32(a, b):
    return jnp.dot(a, b, preferred_element_type=F32)


def ffn_steps(j, n_tiles, n_s, w1_ref, w2_ref, h0, h1, acc, finish):
    def up(h_ref):
        h_ref[...] = jax.nn.gelu(dot32(n_s[...], w1_ref[...])).astype(BF16)

    def down(h_ref):
        acc[...] += dot32(h_ref[...], w2_ref[...])

    @pl.when(j == 0)
    def _():
        up(h0)

    @pl.when((j > 0) & (j < n_tiles) & (j % 2 == 1))
    def _():
        up(h1)
        down(h0)

    @pl.when((j > 0) & (j < n_tiles) & (j % 2 == 0))
    def _():
        up(h0)
        down(h1)

    @pl.when(j == n_tiles)
    def _():
        last = h1 if n_tiles % 2 == 0 else h0
        finish(dot32(last[...], w2_ref[...]))


def layers_kernel(n_tiles, x_ref, w1_ref, w2_ref, o_ref, x_s, n_s, h0, h1, acc):
    layer, j = pl.program_id(0), pl.program_id(1)

    @pl.when((layer == 0) & (j == 0))
    def _():
        x_s[...] = x_ref[...]

    @pl.when(j == 0)
    def _():
        n_s[...] = rms(x_s[...].astype(F32)).astype(BF16)
        acc[...] = jnp.zeros_like(acc)

    def finish(last):
        out = (x_s[...].astype(F32) + (acc[...] + last)).astype(BF16)
        x_s[...] = out
        o_ref[...] = out

    ffn_steps(j, n_tiles, n_s, w1_ref, w2_ref, h0, h1, acc, finish)


def run_layers(x_val, w_one, w_two):
    rows, width = x_val.shape
    _, n_layers, _, ffn = w_one.shape
    n_tiles = ffn // FFN_TILE
    whole = pl.BlockSpec((rows, width), lambda l, j: (0, 0))
    return pl.pallas_call(
        functools.partial(layers_kernel, n_tiles),
        out_shape=jax.ShapeDtypeStruct((rows, width), BF16),
        grid=(n_layers, n_tiles + 1),
        in_specs=[
            whole,
            pl.BlockSpec((None, None, width, FFN_TILE), lambda l, j: (0, l, 0, jnp.minimum(j, n_tiles - 1))),
            pl.BlockSpec((None, None, FFN_TILE, width), lambda l, j: (0, l, jnp.maximum(j - 1, 0), 0)),
        ],
        out_specs=whole,
        scratch_shapes=[
            pltpu.VMEM((rows, width), BF16),
            pltpu.VMEM((rows, width), BF16),
            pltpu.VMEM((rows, FFN_TILE), BF16),
            pltpu.VMEM((rows, FFN_TILE), BF16),
            pltpu.VMEM((rows, width), F32),
        ],
        compiler_params=pltpu.CompilerParams(dimension_semantics=("arbitrary", "arbitrary"), vmem_limit_bytes=VMEM_BYTES),
        cost_estimate=pl.CostEstimate(
            flops=4 * rows * width * ffn * n_layers, bytes_accessed=4 * width * ffn * n_layers, transcendentals=0
        ),
        name="layers",
    )(x_val, w_one, w_two)


def mtp_kernel(
    n_proj, n_tiles, h_ref, e_ref, gf_ref, gh_ref, ge_ref, gm_ref, wp_ref, w1_ref, w2_ref, o_ref,
    cat_s, z_s, n_s, h0, h1, acc,
):
    step = pl.program_id(0)
    rows, width = h_ref.shape
    proj_tile = wp_ref.shape[0]

    @pl.when(step == 0)
    def _():
        cat_s[:, :width] = rms_gain(h_ref[...], gh_ref)
        cat_s[:, width:] = rms_gain(e_ref[...], ge_ref)
        o_ref[:rows, :] = rms_gain(h_ref[...], gf_ref)
        acc[...] = jnp.zeros_like(acc)

    for k in range(n_proj):
        @pl.when(step == k)
        def _():
            acc[...] += dot32(cat_s[:, k * proj_tile:(k + 1) * proj_tile], wp_ref[...])

    @pl.when(step == n_proj - 1)
    def _():
        z_s[...] = acc[...].astype(BF16)
        n_s[...] = rms_gain(z_s[...], gm_ref)
        acc[...] = jnp.zeros_like(acc)

    def finish(last):
        z_new = (z_s[...].astype(F32) + (acc[...] + last)).astype(BF16)
        o_ref[rows:, :] = rms_gain(z_new, gf_ref)

    ffn_steps(step - n_proj, n_tiles, n_s, w1_ref, w2_ref, h0, h1, acc, finish)


def run_mtp(h_last, e_rows, gain_f, gain_h, gain_e, gain_m, w_proj, u_one, u_two):
    rows, width = h_last.shape
    ffn = u_one.shape[1]
    n_tiles = ffn // FFN_TILE
    n_proj = w_proj.shape[0] // FFN_TILE
    whole = pl.BlockSpec((rows, width), lambda s: (0, 0))
    gain = pl.BlockSpec((1, width), lambda s: (0, 0))
    return pl.pallas_call(
        functools.partial(mtp_kernel, n_proj, n_tiles),
        out_shape=jax.ShapeDtypeStruct((2 * rows, width), BF16),
        grid=(n_proj + n_tiles + 1,),
        in_specs=[
            whole, whole, gain, gain, gain, gain,
            pl.BlockSpec((FFN_TILE, width), lambda s: (jnp.minimum(s, n_proj - 1), 0)),
            pl.BlockSpec((width, FFN_TILE), lambda s: (0, jnp.clip(s - n_proj, 0, n_tiles - 1))),
            pl.BlockSpec((FFN_TILE, width), lambda s: (jnp.clip(s - n_proj - 1, 0, n_tiles - 1), 0)),
        ],
        out_specs=pl.BlockSpec((2 * rows, width), lambda s: (0, 0)),
        scratch_shapes=[
            pltpu.VMEM((rows, 2 * width), BF16),
            pltpu.VMEM((rows, width), BF16),
            pltpu.VMEM((rows, width), BF16),
            pltpu.VMEM((rows, FFN_TILE), BF16),
            pltpu.VMEM((rows, FFN_TILE), BF16),
            pltpu.VMEM((rows, width), F32),
        ],
        compiler_params=pltpu.CompilerParams(dimension_semantics=("arbitrary",), vmem_limit_bytes=VMEM_BYTES),
        cost_estimate=pl.CostEstimate(
            flops=4 * rows * width * (ffn + width), bytes_accessed=4 * width * (ffn + width), transcendentals=0
        ),
        name="mtp",
    )(h_last, e_rows, gain_f[None], gain_h[None], gain_e[None], gain_m[None], w_proj, u_one, u_two)


LANES = 128
GROUP = 16


def head_stats(buf, n_cols, base, tgt_ref, m_ref, s_ref, p_ref):
    rows = buf.shape[0]
    lane = lax.broadcasted_iota(jnp.int32, (GROUP, LANES), 1)
    for r in range(0, rows, GROUP):
        rs = slice(r, r + GROUP)
        parts = [buf[rs, c:c + LANES] for c in range(0, n_cols, LANES)]
        top = parts[0]
        for part in parts[1:]:
            top = jnp.maximum(top, part)
        m_old = m_ref[rs, :]
        m_new = jnp.maximum(m_old, top)
        total = s_ref[rs, :] * jnp.exp(m_old - m_new)
        rel = tgt_ref[rs, :] - lane - base
        pick = p_ref[rs, :]
        for k, part in enumerate(parts):
            total = total + jnp.exp(part - m_new)
            pick = jnp.where(rel == k * LANES, part, pick)
        m_ref[rs, :] = m_new
        s_ref[rs, :] = total
        p_ref[rs, :] = pick


def head_kernel(n_steps, tail, x_ref, tgt_ref, w_ref, o_ref, buf_a, buf_b, m_ref, s_ref, p_ref):
    i = pl.program_id(0)
    half = buf_a.shape[1]
    state = (tgt_ref, m_ref, s_ref, p_ref)

    @pl.when(i == 0)
    def _():
        buf_b[...] = jnp.full_like(buf_b, -3e38)
        m_ref[...] = jnp.full_like(m_ref, -3e38)
        s_ref[...] = jnp.zeros_like(s_ref)
        p_ref[...] = jnp.zeros_like(p_ref)

    @pl.when(i < n_steps - 1)
    def _():
        buf_a[...] = dot32(x_ref[...], w_ref[:, :half])
        head_stats(buf_b, half, (2 * i - 1) * half, *state)
        buf_b[...] = dot32(x_ref[...], w_ref[:, half:])
        head_stats(buf_a, half, 2 * i * half, *state)

    @pl.when(i == n_steps - 1)
    def _():
        head_stats(buf_b, half, (2 * i - 1) * half, *state)
        done = 0
        while done < tail:
            cols = min(half, tail - done)
            buf_a[:, :cols] = dot32(x_ref[...], w_ref[:, done:done + cols])
            head_stats(buf_a, cols, 2 * i * half + done, *state)
            done += cols
        top = jnp.max(m_ref[...], axis=1, keepdims=True)
        total = jnp.sum(s_ref[...] * jnp.exp(m_ref[...] - top), axis=1, keepdims=True)
        picked = jnp.sum(p_ref[...], axis=1, keepdims=True)
        o_ref[...] = jnp.broadcast_to(top + jnp.log(total) - picked, o_ref.shape)


def run_head(x_val, targets, w_out):
    rows, width = x_val.shape
    vocab = w_out.shape[1]
    tile = 2 * HEAD_HALF
    n_steps = pl.cdiv(vocab, tile)
    tail = vocab - (n_steps - 1) * tile
    out = pl.pallas_call(
        functools.partial(head_kernel, n_steps, tail),
        out_shape=jax.ShapeDtypeStruct((rows, LANES), F32),
        grid=(n_steps,),
        in_specs=[
            pl.BlockSpec((rows, width), lambda i: (0, 0)),
            pl.BlockSpec((rows, LANES), lambda i: (0, 0)),
            pl.BlockSpec((width, tile), lambda i: (0, i)),
        ],
        out_specs=pl.BlockSpec((rows, LANES), lambda i: (0, 0)),
        scratch_shapes=[
            pltpu.VMEM((rows, HEAD_HALF), F32),
            pltpu.VMEM((rows, HEAD_HALF), F32),
            pltpu.VMEM((rows, LANES), F32),
            pltpu.VMEM((rows, LANES), F32),
            pltpu.VMEM((rows, LANES), F32),
        ],
        compiler_params=pltpu.CompilerParams(dimension_semantics=("arbitrary",), vmem_limit_bytes=VMEM_BYTES),
        cost_estimate=pl.CostEstimate(flops=2 * rows * width * vocab, bytes_accessed=2 * width * vocab, transcendentals=0),
        name="head",
    )(x_val, jnp.broadcast_to(targets[:, None], (rows, LANES)), w_out)
    return out[:, 0]


def solution(mesh):
    n_data = mesh.shape["dp"]
    n_stages = mesh.shape["pp"]

    def flat(dp_idx, pp_idx):
        return dp_idx * n_stages + pp_idx

    def swap_perm(k):
        return [(flat(d, 0), flat(d ^ k, 0)) for d in range(n_data)]

    def fetch_rows(table, ids_all, cap):
        me = lax.axis_index("dp")
        n_local = table.shape[0]
        n = ids_all.shape[1]
        owner = ids_all // n_local
        same = owner[:, :, None] == jnp.arange(n_data)[None, None, :]
        most = jnp.max(jnp.sum(same.astype(jnp.int32), axis=1))
        before = jnp.arange(n)[:, None] < jnp.arange(n)[None, :]
        rank_all = jnp.einsum(
            "dns,nm->dms", same.astype(BF16), before.astype(BF16), preferred_element_type=F32
        ).astype(jnp.int32)
        dests = jnp.bitwise_xor(me, jnp.arange(n_data))
        mine = jnp.take(same, me, axis=2)[dests]
        my_rank = jnp.take(rank_all, me, axis=2)[dests]
        local = (ids_all - me * n_local)[dests]
        own_src = jnp.bitwise_xor(owner[me], me)
        own_rank = jnp.sum(jnp.where(same[me], rank_all[me], 0), axis=1)

        def one_round(j):
            slot = j * cap + jnp.arange(cap)
            hit = mine[:, None, :] & (my_rank[:, None, :] == slot[None, :, None])
            idx = jnp.sum(jnp.where(hit, local[:, None, :], 0), axis=2)
            packed = [table[idx[k]] for k in range(n_data)]
            got = [packed[0]] + [lax.ppermute(packed[k], ("dp", "pp"), swap_perm(k)) for k in range(1, n_data)]
            in_round = (own_rank >= j * cap) & (own_rank < (j + 1) * cap)
            place = jnp.where(in_round, own_src * cap + own_rank - j * cap, -1)
            pick = (place[:, None] == jnp.arange(n_data * cap)[None, :]).astype(BF16)
            return dot32(pick, jnp.concatenate(got, axis=0)).astype(BF16)

        first = one_round(0)
        _, rows = lax.while_loop(
            lambda c: c[0] * cap < most, lambda c: (c[0] + 1, c[1] + one_round(c[0])), (jnp.int32(1), first)
        )
        return rows

    def body(tok_ids, emb_s, w_one, w_two, gain_f, gain_h, gain_e, gain_m, w_proj, u_one, u_two, w_out):
        stage = lax.axis_index("pp")
        n_micro, batch_dev, seq_plus = tok_ids.shape
        seq_len = seq_plus - 2
        n_seq = n_micro * batch_dev
        n_tok = n_seq * seq_len
        rows_a = ROWS_A
        rows_b = n_tok - rows_a
        table = emb_s[0]
        ids = tok_ids.reshape(n_seq, seq_plus)
        want = ids[:, :seq_len + 1].reshape(n_seq * (seq_len + 1))
        ids_all = lax.all_gather(want, "dp")
        cut = rows_a + (rows_a - 1) // seq_len

        rows_lo = fetch_rows(table, ids_all[:, :cut], CAP_A)
        rows_hi = fetch_rows(table, ids_all[:, cut:], CAP_B)

        def tokens(rows, shift):
            return rows.reshape(n_seq, seq_len + 1, -1)[:, shift:shift + seq_len].reshape(n_tok, -1)

        lo_idx = [t + t // seq_len for t in range(rows_a)]
        x_a = jnp.concatenate(
            [rows_lo[s * (seq_len + 1):min(s * (seq_len + 1) + seq_len, cut)] for s in range(n_seq) if s * (seq_len + 1) < cut],
            axis=0,
        )
        assert x_a.shape[0] == len(lo_idx)
        x_a = run_layers(x_a, w_one, w_two)

        all_rows = jnp.concatenate([rows_lo, rows_hi], axis=0)
        x_b = jnp.pad(tokens(all_rows, 0)[rows_a:], ((0, rows_a - rows_b), (0, 0)))
        moved = lax.ppermute(x_a, "pp", [(0, 1)])
        e_all = lax.ppermute(all_rows, "pp", [(0, 1)])
        x_mid = run_layers(jnp.where(stage == 0, x_b, moved), w_one, w_two)
        swapped = lax.ppermute(x_mid, "pp", [(0, 1), (1, 0)])
        e_rows = tokens(jnp.where(stage == 0, all_rows, e_all), 1)
        tgt_main = ids[:, 1:seq_len + 1].reshape(n_tok)
        tgt_mtp = ids[:, 2:].reshape(n_tok)

        def tail(h_last, lo, hi):
            rows = run_mtp(h_last, e_rows[lo:hi], gain_f, gain_h, gain_e, gain_m, w_proj, u_one, u_two)
            nll = run_head(rows, jnp.concatenate([tgt_main[lo:hi], tgt_mtp[lo:hi]]), w_out)
            pad = lambda v: jnp.pad(v, (lo, n_tok - hi))
            return pad(nll[:hi - lo]), pad(nll[hi - lo:])

        def tail_first(swapped):
            return tail(swapped, 0, rows_a)

        def tail_last(swapped):
            return tail(run_layers(swapped[:rows_b], w_one, w_two), rows_a, n_tok)

        main_part, mtp_part = lax.cond(stage == 0, tail_first, tail_last, swapped)
        local_sum = jnp.sum(main_part) + MTP_WEIGHT * jnp.sum(mtp_part)
        main_nll = lax.psum(main_part, "pp").reshape(n_micro, batch_dev, seq_len)
        mtp_nll = lax.psum(mtp_part, "pp").reshape(n_micro, batch_dev, seq_len)
        total_loss = lax.psum(local_sum, ("dp", "pp")) / (n_tok * n_data)
        return total_loss, main_nll, mtp_nll

    rep = P()
    in_specs = (P(None, "dp", None), P("pp", "dp", None), P("pp"), P("pp")) + (rep,) * 8
    out_specs = (rep, P(None, "dp", None), P(None, "dp", None))
    return jax.shard_map(body, mesh=mesh, in_specs=in_specs, out_specs=out_specs, check_vma=False)
```

time: 4820 us -> 561 us (0.12)
  waiting for transfers between devices: 3180 us -> 3.62 us
  starting transfers between devices: 684 us -> 28.5 us
  blocking collectives: 667 us -> 37 us
  Pallas kernels: 0 us -> 394 us
  matrix products: 190 us -> 5.14 us
    all_gather x1 -> x0, waiting for transfers between devices: 3170 us -> none  [body(): table = lax.all_gather(emb_s[0], 'dp', axis=0, tiled=True)]
    ppermute x6 -> x9, starting transfers between devices: 684 us -> 28.5 us  [the longest x6 20.4 us: one_round(): lax.ppermute(packed[k], ('dp', 'pp'), swap_perm(k))]
    psum x2, blocking collectives: 667 us -> 27 us  [the longest x1 23.8 us: body(): total_loss = lax.psum(local_sum, ('dp', 'pp')) / (n_tok * n_data)]
    pallas_call x0 -> x4, Pallas kernels: none -> 394 us  [the longest x1 236 us: run_head(): pl.pallas_call(functools.partial(head_kernel, n_steps, tail), out_shape=j...]
    dot_general x9 -> x4, matrix products: 190 us -> 5.14 us  [the longest x2 4.82 us: dot32(): return jnp.dot(a, b, preferred_element_type=F32)]
  transfers between devices with their start and end apart: 7 -> 9, of which waited for: 1 -> 1; matrix products, arithmetic and copies ran while one was open for 4% -> 9% of each run, Pallas kernels for 0% -> 11%
where the time goes in v1:
time: 561 us; the launch traced here: 552 us
  Pallas kernels  394 us (70%)
  local copies, waits for them, and re-layouts  54.2 us (10%)
  blocking collectives  37 us (7%)
  starting transfers between devices  28.5 us (5%)
  other arithmetic  12.7 us (2%)
  loops' own time  11.5 us (2%)
    pallas_call x1, Pallas kernels, run_head(): pl.pallas_call(functools.partial(head_kernel, n_steps, tail), out_shape=j...  236 us
    pallas_call x2, Pallas kernels, run_layers(): pl.pallas_call(functools.partial(layers_kernel, n_tiles), out_shape=jax.S...  117 us
    pallas_call x1, Pallas kernels, run_mtp(): pl.pallas_call(functools.partial(mtp_kernel, n_proj, n_tiles), out_shape=...  41 us
    gather x8, local copies, waits for them, and re-layouts, one_round(): packed = [table[idx[k]] for k in range(n_data)]  34.8 us
    psum x1, blocking collectives, body(): total_loss = lax.psum(local_sum, ('dp', 'pp')) / (n_tok * n_data)  23.8 us
    ppermute x6, starting transfers between devices, one_round(): lax.ppermute(packed[k], ('dp', 'pp'), swap_perm(k))  20.4 us
  transfers between devices with their start and end apart: 9, of which 1 were waited for; matrix products, arithmetic and copies ran while one was open for 9% of the time, Pallas kernels for 11%

profile of v1, /device:TPU:0, one launch (start us, length us, event | category | flops | bytes accessed | tf_op | source)
XLA Modules:
  0.0 551.6 jit_solution(722830088464613923)
XLA Ops:
  0.7 0.7 reshape.588
  1.4 10.0 %all-gather = s32[4,1,516]{2,1,0:T(1,128)S(1)} all-gather(s32[1,1,516]{2,1,0:T(1,128)S(1)} %reshape.900), channel_id=1, replica_groups=mesh['dp'=4,'pp'=2] {'dp'}, dimensions={0}, use_global_device_ids=true | all-gather | bytes 10320 | tf_op jit(solution)/shard_map/all_gather | solution.py:325
  13.8 4.4 gather_fusion.20
  18.2 3.1 collective-permute-start.10
  21.3 4.3 gather_fusion.21
  25.6 3.9 collective-permute-start.11
  29.6 4.2 gather_fusion.19
  33.8 3.0 collective-permute-start.9
  39.4 1.6 select_reduce_fusion.2
  41.0 4.5 gather_fusion.12
  45.5 2.3 collective-permute-start.6
  48.0 5.6 %gather_fusion.18 = bf16[88,2048]{1,0:T(8,128)(2,1)} fusion(bf16[23136,2048]{1,0:T(8,128)(2,1)} %bitcast.17, s32[1024]{0:T(1024)S(1)} %pad_clamp_fusion.11), kind=kCustom, calls=%fused_computation.18 | custom fusion | bytes 721248 | tf_op jit(solution)/shard_map/gather | solution.py:301
  53.6 4.1 gather_fusion.13
  57.7 3.8 gather_fusion.14
  61.5 3.8 gather_fusion.11
  65.4 0.7 reduce_max.19
  66.1 0.6 reduce_max.18
  66.8 3.1 collective-permute-start.7
  69.8 4.9 collective-permute-start.8
  74.8 3.0 convolution_convert_fusion.3
  77.8 3.6 collective-permute-done.7
  81.4 1.9 convolution_convert_fusion.2
  83.2 0.9 while.24
  84.3 1.1 pad_maximum_fusion.1.x_ref
  85.4 58.5 %layers.4 = bf16[288,2048]{1,0:T(8,128)(2,1)} custom-call(bf16[288,2048]{1,0:T(8,128)(2,1)} %pad_maximum_fusion.1.x_ref, bf16[1,2,2048,8192]{3,2,1,0:T(8,128)(2,1)} %w1_ref.3, bf16[1,2,8192,2048]{3,2,1,0:T(8,128)(2,1)} %w2_ref.3), custom_call_target="tpu_custom_call" | custom-call | flops 38654705664 | bytes 134217728 | tf_op jit(solution)/shard_map/layers/pallas_call | solution.py:87
  143.9 2.3 collective-permute-start.12
  146.2 1.2 while.25
  147.4 1.6 pad_maximum_fusion
  149.0 5.8 %collective-permute-start.14 = (bf16[516,2048]{1,0:T(8,128)(2,1)S(1)}, bf16[516,2048]{1,0:T(8,128)(2,1)}, u32[]{:S(2)}, u32[]{:S(2)}) collective-permute-start(bf16[516,2048]{1,0:T(8,128)(2,1)S(1)} %pad_maximum_fusion), channel_id=1, source_target_pairs={{0,1},{2,3},{4,5},{6,7}} | collective-permute-start | bytes 6340616 | tf_op jit(solution)/shard_map/ppermute | solution.py:345
  154.8 2.0 reshape.589
  156.7 1.6 slice-done
  158.4 1.4 pad_select_fusion.x_ref
  159.8 58.5 %layers.5 = bf16[288,2048]{1,0:T(8,128)(2,1)} custom-call(bf16[288,2048]{1,0:T(8,128)(2,1)} %pad_select_fusion.x_ref, bf16[1,2,2048,8192]{3,2,1,0:T(8,128)(2,1)} %w1_ref.3, bf16[1,2,8192,2048]{3,2,1,0:T(8,128)(2,1)} %w2_ref.3), custom_call_target="tpu_custom_call" | custom-call | flops 38654705664 | bytes 134217728 | tf_op jit(solution)/shard_map/layers/pallas_call | solution.py:87
  218.4 2.1 broadcast_select_fusion
  220.6 2.0 reshape.591
  222.5 2.2 slice.248
  224.8 293.5 %conditional.1 = (f32[512]{0:T(512)}, f32[512]{0:T(512)}, f32[]{:T(128)}) conditional(s32[]{:T(128)} %convert_element_type.49, (bf16[288,2048]{1,0:T(8,128)(2,1)}, bf16[1,2,2048,8192]{3,2,1,0:T(8,128)(2,1)}, bf16[1,2,8192,2048]{3,2,1,0:T(8,128)(2,1)}, bf16[512,2048]{1,0:T(8,128)(2,1)S(1)}, bf16[2048]{0:T(1024)(128)(2,1)S(1)}, ...), branch_computations={%region_14.15_spmd, %region_15.16_spmd} | conditional | flops 242497880064 | bytes 601114624 | solution.py:364
  233.9 1.1 slice.114.e_ref
  235.0 0.6 broadcast_in_dim.115.gf_ref
  236.2 0.6 broadcast_in_dim.117.ge_ref
  237.4 41.0 %mtp.3.x_ref = bf16[576,2048]{1,0:T(8,128)(2,1)} custom-call(bf16[288,2048]{1,0:T(8,128)(2,1)} %get-tuple-element.187.h_ref, bf16[288,2048]{1,0:T(8,128)(2,1)} %slice.114.e_ref, bf16[1,2048]{1,0:T(2,128)(2,1)} %broadcast_in_dim.115.gf_ref, bf16[1,2048]{1,0:T(2,128)(2,1)} %broadcast_in_dim.116.gh_ref, bf16[1,2048]{1,0:T(2,128)(2,1)} %broadcast_in_dim.117.ge_ref, ...), custom_call_target="tpu_custom_call" | custom-call | flops 24159191040 | bytes 83886080 | tf_op jit(solution)/shard_map/cond/branch_1_fun/mtp/pallas_call | solution.py:152
  278.5 0.9 broadcast_in_dim.119.tgt_ref
  279.3 236.3 %head.5 = f32[576,128]{1,0:T(8,128)} custom-call(bf16[576,2048]{1,0:T(8,128)(2,1)} %mtp.3.x_ref, s32[576,128]{1,0:T(8,128)} %broadcast_in_dim.119.tgt_ref, bf16[2048,92544]{1,0:T(8,128)(2,1)} %get-tuple-element.198.w_ref), custom_call_target="tpu_custom_call" | custom-call | flops 218338689024 | bytes 379060224 | tf_op jit(solution)/shard_map/cond/branch_1_fun/head/pallas_call | solution.py:245
  515.7 1.2 slice_reduce_fusion.2
  518.3 1.4 reduce_sum.103
  519.7 1.3 reduce_sum.102
  522.3 23.8 %psum.21 = f32[]{:T(128)} all-reduce(f32[]{:T(128)S(6)} %add.286), channel_id=1, replica_groups=mesh['dp'=4,'pp'=2] {'dp','pp'}, use_global_device_ids=true, to_apply=%region_18.19 | all-reduce | flops 1 | bytes 8 | tf_op jit(solution)/shard_map/psum | solution.py:368
  546.1 3.2 all-reduce.5
  (75 shorter events, 7.9 us)
Async XLA Ops:
  1.4 10.1 %copy-start = (s32[4,130]{1,0:T(4,128)}, s32[4,130]{1,0:T(4,128)S(1)}, u32[]{:S(2)}) copy-start(s32[4,130]{1,0:T(4,128)S(1)} %reshape.588) | copy-start | bytes 6244
  18.2 51.7 %collective-permute-start.10 = (bf16[88,2048]{1,0:T(8,128)(2,1)S(1)}, bf16[88,2048]{1,0:T(8,128)(2,1)}, u32[]{:S(2)}, u32[]{:S(2)}) collective-permute-start(bf16[88,2048]{1,0:T(8,128)(2,1)S(1)} %gather_fusion.20), channel_id=1, source_target_pairs={{0,4},{2,6},{4,0},{6,2}} | collective-permute-start | bytes 1081352 | tf_op jit(solution)/shard_map/ppermute | solution.py:302
  25.6 49.2 %collective-permute-start.11 = (bf16[88,2048]{1,0:T(8,128)(2,1)S(1)}, bf16[88,2048]{1,0:T(8,128)(2,1)}, u32[]{:S(2)}, u32[]{:S(2)}) collective-permute-start(bf16[88,2048]{1,0:T(8,128)(2,1)S(1)} %gather_fusion.21), channel_id=1, source_target_pairs={{0,6},{2,4},{4,2},{6,0}} | collective-permute-start | bytes 1081352 | tf_op jit(solution)/shard_map/ppermute | solution.py:302
  33.8 41.0 %collective-permute-start.9 = (bf16[88,2048]{1,0:T(8,128)(2,1)S(1)}, bf16[88,2048]{1,0:T(8,128)(2,1)}, u32[]{:S(2)}, u32[]{:S(2)}) collective-permute-start(bf16[88,2048]{1,0:T(8,128)(2,1)S(1)} %gather_fusion.19), channel_id=1, source_target_pairs={{0,2},{2,0},{4,6},{6,4}} | collective-permute-start | bytes 1081352 | tf_op jit(solution)/shard_map/ppermute | solution.py:302
  45.5 32.3 %collective-permute-start.6 = (bf16[104,2048]{1,0:T(8,128)(2,1)S(1)}, bf16[104,2048]{1,0:T(8,128)(2,1)}, u32[]{:S(2)}, u32[]{:S(2)}) collective-permute-start(bf16[104,2048]{1,0:T(8,128)(2,1)S(1)} %gather_fusion.12), channel_id=1, source_target_pairs={{0,2},{2,0},{4,6},{6,4}} | collective-permute-start | bytes 1277960 | tf_op jit(solution)/shard_map/ppermute | solution.py:302
  66.8 14.6 %collective-permute-start.7 = (bf16[104,2048]{1,0:T(8,128)(2,1)S(1)}, bf16[104,2048]{1,0:T(8,128)(2,1)S(1)}, u32[]{:S(2)}, u32[]{:S(2)}) collective-permute-start(bf16[104,2048]{1,0:T(8,128)(2,1)S(1)} %gather_fusion.13), channel_id=1, source_target_pairs={{0,4},{2,6},{4,0},{6,2}} | collective-permute-start | bytes 1277960 | tf_op jit(solution)/shard_map/ppermute | solution.py:302
  69.8 11.5 %collective-permute-start.8 = (bf16[104,2048]{1,0:T(8,128)(2,1)S(1)}, bf16[104,2048]{1,0:T(8,128)(2,1)S(1)}, u32[]{:S(2)}, u32[]{:S(2)}) collective-permute-start(bf16[104,2048]{1,0:T(8,128)(2,1)S(1)} %gather_fusion.14), channel_id=1, source_target_pairs={{0,6},{2,4},{4,2},{6,0}} | collective-permute-start | bytes 1277960 | tf_op jit(solution)/shard_map/ppermute | solution.py:302
  143.9 14.5 %collective-permute-start.12 = (bf16[288,2048]{1,0:T(8,128)(2,1)}, bf16[288,2048]{1,0:T(8,128)(2,1)}, u32[]{:S(2)}, u32[]{:S(2)}) collective-permute-start(bf16[288,2048]{1,0:T(8,128)(2,1)} %layers.4), channel_id=1, source_target_pairs={{0,1},{2,3},{4,5},{6,7}} | collective-permute-start | bytes 3538952 | tf_op jit(solution)/shard_map/ppermute | solution.py:344
  149.0 69.4 %collective-permute-start.14 = (bf16[516,2048]{1,0:T(8,128)(2,1)S(1)}, bf16[516,2048]{1,0:T(8,128)(2,1)}, u32[]{:S(2)}, u32[]{:S(2)}) collective-permute-start(bf16[516,2048]{1,0:T(8,128)(2,1)S(1)} %pad_maximum_fusion), channel_id=1, source_target_pairs={{0,1},{2,3},{4,5},{6,7}} | collective-permute-start | bytes 6340616 | tf_op jit(solution)/shard_map/ppermute | solution.py:345
  156.7 1.6 slice-start
  159.8 58.5 %copy-start.1 = (s32[4,130]{1,0:T(4,128)S(1)}, s32[4,130]{1,0:T(4,128)}, u32[]{:S(2)}) copy-start(s32[4,130]{1,0:T(4,128)} %copy-done) | copy-start | bytes 6244
  218.3 6.4 %collective-permute-start.13 = (bf16[288,2048]{1,0:T(8,128)(2,1)}, bf16[288,2048]{1,0:T(8,128)(2,1)}, u32[]{:S(2)}, u32[]{:S(2)}) collective-permute-start(bf16[288,2048]{1,0:T(8,128)(2,1)} %layers.5), channel_id=1, source_target_pairs={{0,1},{1,0},{2,3},{3,2},{4,5},{5,4},{6,7},{7,6}} | collective-permute-start | bytes 3538952 | tf_op jit(solution)/shard_map/ppermute | solution.py:347
  222.5 2.2 copy-start.2
  222.5 2.2 copy-start.3
  222.5 2.2 copy-start.4
  222.5 2.3 copy-start.5

commit v2 on v1

v2 whole, which is shorter than its diff:
```python
import functools

import jax
import jax.numpy as jnp
from jax import lax
from jax.experimental import pallas as pl
from jax.experimental.pallas import tpu as pltpu
from jax.sharding import PartitionSpec as P

NORM_EPS = 1e-6
MTP_WEIGHT = 0.3
F32 = jnp.float32
BF16 = jnp.bfloat16
I32 = jnp.int32
MESH = pl.DeviceIdType.MESH
VMEM_BYTES = 60 * 1024 * 1024
LANES = 128
GROUP = 16

ROWS_A = 288
FFN_TILE = 1024
HEAD_HALF = 1024
CAP = 176
BLOCK = 8


def rms(x_f):
    return x_f * lax.rsqrt(jnp.mean(x_f * x_f, axis=-1, keepdims=True) + NORM_EPS)


def rms_gain(x_val, gain_ref):
    return (rms(x_val.astype(F32)) * gain_ref[...].astype(F32)).astype(BF16)


def dot32(a, b):
    return jnp.dot(a, b, preferred_element_type=F32)


def norm_rows(dst, src, gain_ref=None, base=0):
    for r in range(0, src.shape[0], GROUP):
        val = rms(src[r:r + GROUP, :].astype(F32))
        if gain_ref is not None:
            val = val * gain_ref[...].astype(F32)
        dst[base + r:base + r + GROUP, :] = val.astype(BF16)


def collective(idx):
    return pltpu.CompilerParams(collective_id=idx, has_side_effects=True, vmem_limit_bytes=VMEM_BYTES)


def enter(peers):
    barrier = pltpu.get_barrier_semaphore()
    for peer in peers:
        pl.semaphore_signal(barrier, inc=1, device_id=peer, device_id_type=MESH)
    pl.semaphore_wait(barrier, len(peers))


def push(src, dst, send_sem, recv_sem, peer):
    return pltpu.make_async_remote_copy(
        src_ref=src, dst_ref=dst, send_sem=send_sem, recv_sem=recv_sem, device_id=peer, device_id_type=MESH
    )


def slot_ranks(held):
    row = lax.broadcasted_iota(I32, (LANES, LANES), 0)
    col = lax.broadcasted_iota(I32, (LANES, LANES), 1)
    ahead = dot32(held.astype(BF16), (row < col).astype(BF16))
    total = dot32(held.astype(BF16), jnp.ones((LANES, LANES), BF16))
    out, base = [], jnp.zeros((1, LANES), F32)
    for r in range(held.shape[0]):
        out.append(ahead[r:r + 1, :] + base)
        base = base + total[r:r + 1, :]
    return jnp.concatenate(out, axis=0)


def slots_kernel(n_data, n_local, ids_ref, idx_ref, most_ref, got, send_sem, recv_sem):
    me, stage = lax.axis_index("dp"), lax.axis_index("pp")
    peers = [(jnp.bitwise_xor(me, k), stage) for k in range(1, n_data)]
    enter(peers)
    copies = [push(ids_ref, got.at[k], send_sem.at[k], recv_sem.at[k], peer) for k, peer in enumerate(peers)]
    for copy in copies:
        copy.start()
    for copy in copies:
        copy.wait()
    most = jnp.zeros((1, 1), F32)
    slot = lax.broadcasted_iota(I32, (CAP, LANES), 0).astype(F32)
    for k in range(n_data):
        ids = ids_ref[...] if k == 0 else got[k - 1]
        for s in range(n_data):
            inside = ((ids >= s * n_local) & (ids < (s + 1) * n_local)).astype(F32)
            most = jnp.maximum(most, jnp.sum(jnp.sum(inside, axis=1, keepdims=True), axis=0, keepdims=True))
        local = ids - me * n_local
        held = ((local >= 0) & (local < n_local)).astype(F32)
        rank = jnp.where(held > 0, slot_ranks(held), -1.0)
        high = lax.shift_right_arithmetic(local, 8)
        low = (local - high * 256).astype(F32)
        high = high.astype(F32)
        acc = jnp.zeros((BLOCK, CAP), F32)
        for r in range(ids.shape[0]):
            hit = (jnp.broadcast_to(rank[r:r + 1, :], (CAP, LANES)) == slot).astype(BF16)
            keep = held[r:r + 1, :]
            pair = jnp.concatenate(
                [high[r:r + 1, :] * keep, low[r:r + 1, :] * keep, jnp.zeros((BLOCK - 2, LANES), F32)], axis=0
            ).astype(BF16)
            acc = acc + lax.dot_general(pair, hit, (((1,), (1,)), ((), ())), preferred_element_type=F32)
        idx_ref[k:k + 1, :CAP] = (acc[0:1, :] * 256.0 + acc[1:2, :]).astype(I32)
    most_ref[...] = jnp.broadcast_to(most, most_ref.shape).astype(I32)


def run_slots(ids_tile, n_data, n_local):
    vmem = pl.BlockSpec(memory_space=pltpu.VMEM)
    return pl.pallas_call(
        functools.partial(slots_kernel, n_data, n_local),
        out_shape=[jax.ShapeDtypeStruct((n_data, 2 * LANES), I32), jax.ShapeDtypeStruct((BLOCK, LANES), I32)],
        in_specs=[vmem],
        out_specs=[vmem, vmem],
        scratch_shapes=[
            pltpu.VMEM((n_data - 1, BLOCK, LANES), I32),
            pltpu.SemaphoreType.DMA((n_data - 1,)),
            pltpu.SemaphoreType.DMA((n_data - 1,)),
        ],
        compiler_params=collective(0),
        name="slots",
    )(ids_tile)


def pack_kernel(n_data, idx_ref, lane_ref, table_ref, o_ref, held, sems):
    parts = [(0, LANES), (LANES, CAP - LANES)]

    @pl.when(lax.axis_index("pp") == 0)
    def _():
        for k in range(n_data):
            for p, (first, count) in enumerate(parts):
                def fetch(c, carry):
                    start = pl.multiple_of(lax.shift_right_logical(idx_ref[k, first + c], 3) * BLOCK, BLOCK)
                    to = pl.multiple_of((k * CAP + first + c) * BLOCK, BLOCK)
                    pltpu.make_async_copy(
                        table_ref.at[pl.ds(start, BLOCK), :], held.at[pl.ds(to, BLOCK), :], sems.at[k * 2 + p]
                    ).start()
                    return carry

                lax.fori_loop(0, count, fetch, 0, unroll=8)
        for k in range(n_data):
            for p, (first, count) in enumerate(parts):
                at = (k * CAP + first) * BLOCK
                span = count * BLOCK
                pltpu.make_async_copy(table_ref.at[pl.ds(0, span), :], held.at[pl.ds(at, span), :], sems.at[k * 2 + p]).wait()
                idx = jnp.broadcast_to(lane_ref[k:k + 1, p * LANES:(p + 1) * LANES].astype(F32), (LANES, LANES))
                idx = jnp.transpose(idx)[:count, :].astype(I32)
                low = jnp.bitwise_and(idx, BLOCK - 1)
                row = lax.broadcasted_iota(I32, (count, LANES), 0)
                lane = lax.broadcasted_iota(I32, (count, LANES), 1)
                picks = []
                for c in range(0, span, LANES):
                    at_row = c // BLOCK + lax.shift_right_logical(lane, 3)
                    picks.append(((row == at_row) & (low == jnp.bitwise_and(lane, BLOCK - 1))).astype(F32).astype(BF16))
                pick = jnp.concatenate(picks, axis=1)
                o_ref[k, first:first + count, :] = dot32(pick, held[at:at + span, :]).astype(BF16)


def run_pack(idx, table):
    n_data = idx.shape[0]
    width = table.shape[1]
    return pl.pallas_call(
        functools.partial(pack_kernel, n_data),
        out_shape=jax.ShapeDtypeStruct((n_data, CAP, width), BF16),
        in_specs=[
            pl.BlockSpec(memory_space=pltpu.SMEM),
            pl.BlockSpec(memory_space=pltpu.VMEM),
            pl.BlockSpec(memory_space=pl.ANY),
        ],
        out_specs=pl.BlockSpec(memory_space=pltpu.VMEM),
        scratch_shapes=[pltpu.VMEM((n_data * CAP * BLOCK, width), BF16), pltpu.SemaphoreType.DMA((2 * n_data,))],
        compiler_params=pltpu.CompilerParams(vmem_limit_bytes=VMEM_BYTES),
        name="pack",
    )(idx, idx, table)


def trade_kernel(n_data, n_local, n_seq, ids_ref, packed_ref, x_ref, e_ref, got, pick_s, send_sem, recv_sem):
    me, stage = lax.axis_index("dp"), lax.axis_index("pp")
    n_tok = n_seq * LANES
    if x_ref.shape[0] > n_tok:
        x_ref[n_tok:, :] = jnp.zeros((x_ref.shape[0] - n_tok, x_ref.shape[1]), BF16)

    @pl.when(stage == 0)
    def _():
        peers = [(jnp.bitwise_xor(me, k), stage) for k in range(1, n_data)]
        enter(peers)
        copies = [
            push(packed_ref.at[k + 1], got.at[k], send_sem.at[k], recv_sem.at[k], peer) for k, peer in enumerate(peers)
        ]
        for k in (2, 0, 1):
            copies[k].start()
        ids = ids_ref[...]
        slot = lax.broadcasted_iota(I32, (CAP, LANES), 0).astype(F32)
        lane = lax.broadcasted_iota(I32, (1, LANES), 1)
        for k in range(n_data):
            src = jnp.bitwise_xor(me, k)
            held = ((ids >= src * n_local) & (ids < (src + 1) * n_local)).astype(F32)
            rank = jnp.where(held > 0, slot_ranks(held), -1.0)
            ahead = pltpu.roll(rank, LANES - 1, 1)
            for s in range(n_seq):
                now = rank[2 * s:2 * s + 1, :]
                later = jnp.where(lane == LANES - 1, ahead[2 * s + 1:2 * s + 2, :], ahead[2 * s:2 * s + 1, :])
                for q, want in ((s, now), (n_seq + s, later)):
                    hit = (jnp.broadcast_to(want, (CAP, LANES)) == slot).astype(F32).astype(BF16)
                    pick_s[k * CAP:(k + 1) * CAP, q * LANES:(q + 1) * LANES] = hit

        def placed(k, block):
            return lax.dot_general(
                pick_s[k * CAP:(k + 1) * CAP, :], block, (((0,), (0,)), ((), ())), preferred_element_type=F32
            ).astype(BF16)

        def add(val):
            x_ref[:n_tok, :] += val[:n_tok]
            e_ref[:n_tok, :] += val[n_tok:]

        first = placed(0, packed_ref[0])
        x_ref[:n_tok, :] = first[:n_tok]
        e_ref[:n_tok, :] = first[n_tok:]
        for k in range(n_data - 1):
            copies[k].wait()
            add(placed(k + 1, got[k]))

    @pl.when(stage != 0)
    def _():
        x_ref[:n_tok, :] = jnp.zeros((n_tok, x_ref.shape[1]), BF16)
        e_ref[:n_tok, :] = jnp.zeros((n_tok, x_ref.shape[1]), BF16)


def run_trade(ids_tile, packed, n_local, n_seq, pad_rows):
    n_data, _, width = packed.shape
    n_tok = n_seq * LANES
    vmem = pl.BlockSpec(memory_space=pltpu.VMEM)
    return pl.pallas_call(
        functools.partial(trade_kernel, n_data, n_local, n_seq),
        out_shape=[jax.ShapeDtypeStruct((pad_rows, width), BF16), jax.ShapeDtypeStruct((n_tok, width), BF16)],
        in_specs=[vmem, vmem],
        out_specs=[vmem, vmem],
        scratch_shapes=[
            pltpu.VMEM((n_data - 1, CAP, width), BF16),
            pltpu.VMEM((n_data * CAP, 2 * n_tok), BF16),
            pltpu.SemaphoreType.DMA((n_data - 1,)),
            pltpu.SemaphoreType.DMA((n_data - 1,)),
        ],
        compiler_params=collective(1),
        name="trade",
    )(ids_tile, packed)


def hand_on_kernel(rows_a, x_ref, e_ref, x_out, e_out, send_sem, recv_sem):
    me, stage = lax.axis_index("dp"), lax.axis_index("pp")
    peer = (me, 1 - stage)
    enter([peer])
    copies = [
        push(x_ref, x_out, send_sem.at[0], recv_sem.at[0], peer),
        push(e_ref.at[pl.ds(rows_a, e_out.shape[0]), :], e_out, send_sem.at[1], recv_sem.at[1], peer),
    ]

    @pl.when(stage == 0)
    def _():
        for copy in copies:
            copy.start()
        for copy in copies:
            copy.wait_send()

    @pl.when(stage != 0)
    def _():
        for copy in copies:
            copy.wait_recv()


def run_hand_on(x_val, e_val):
    rows_a, width = x_val.shape
    rows_b = e_val.shape[0] - rows_a
    hbm = pl.BlockSpec(memory_space=pl.ANY)
    return pl.pallas_call(
        functools.partial(hand_on_kernel, rows_a),
        out_shape=[jax.ShapeDtypeStruct((rows_a, width), BF16), jax.ShapeDtypeStruct((rows_b, width), BF16)],
        in_specs=[hbm, hbm],
        out_specs=[hbm, hbm],
        scratch_shapes=[pltpu.SemaphoreType.DMA((2,)), pltpu.SemaphoreType.DMA((2,))],
        compiler_params=collective(2),
        name="hand_on",
    )(x_val, e_val)


def swap_kernel(x_ref, o_ref, send_sem, recv_sem):
    peer = (lax.axis_index("dp"), 1 - lax.axis_index("pp"))
    enter([peer])
    copy = push(x_ref, o_ref, send_sem, recv_sem, peer)
    copy.start()
    copy.wait()


def run_swap(x_val):
    hbm = pl.BlockSpec(memory_space=pl.ANY)
    return pl.pallas_call(
        swap_kernel,
        out_shape=jax.ShapeDtypeStruct(x_val.shape, BF16),
        in_specs=[hbm],
        out_specs=hbm,
        scratch_shapes=[pltpu.SemaphoreType.DMA, pltpu.SemaphoreType.DMA],
        compiler_params=collective(3),
        name="swap",
    )(x_val)


def finish_kernel(n_data, n_stages, scale, x_ref, nll_ref, total_ref, got, send_sem, recv_sem):
    me, stage = lax.axis_index("dp"), lax.axis_index("pp")
    mine = me * n_stages + stage
    steps = [(k, c) for k in range(n_data) for c in range(n_stages) if (k, c) != (0, 0)]
    peers = [(jnp.bitwise_xor(me, k), jnp.bitwise_xor(stage, c)) for k, c in steps]
    enter(peers)
    copies = [push(x_ref, got.at[mine], send_sem.at[i], recv_sem.at[i], peer) for i, peer in enumerate(peers)]
    for copy in copies:
        copy.start()
    for copy in copies:
        copy.wait()
    got[mine] = x_ref[...]
    half = x_ref.shape[0] // 2
    total = jnp.zeros(x_ref.shape, F32)
    for i in range(n_data * n_stages):
        total = total + got[i]
    main = jnp.sum(jnp.sum(total[:half], axis=1, keepdims=True), axis=0, keepdims=True)
    mtp = jnp.sum(jnp.sum(total[half:], axis=1, keepdims=True), axis=0, keepdims=True)
    total_ref[...] = jnp.broadcast_to((main + MTP_WEIGHT * mtp) * scale, total_ref.shape)
    nll = x_ref[...]
    for c in range(1, n_stages):
        nll = nll + got[me * n_stages + jnp.bitwise_xor(stage, c)]
    nll_ref[...] = nll


def run_finish(tile, n_data, n_stages, scale):
    vmem = pl.BlockSpec(memory_space=pltpu.VMEM)
    n_peers = n_data * n_stages - 1
    return pl.pallas_call(
        functools.partial(finish_kernel, n_data, n_stages, scale),
        out_shape=[jax.ShapeDtypeStruct(tile.shape, F32), jax.ShapeDtypeStruct(tile.shape, F32)],
        in_specs=[vmem],
        out_specs=[vmem, vmem],
        scratch_shapes=[
            pltpu.VMEM((n_data * n_stages,) + tile.shape, F32),
            pltpu.SemaphoreType.DMA((n_peers,)),
            pltpu.SemaphoreType.DMA((n_peers,)),
        ],
        compiler_params=collective(4),
        name="finish",
    )(tile)


def ffn_steps(j, n_tiles, n_s, w1_ref, w2_ref, raw, hid, acc, finish):
    def activate():
        for r in range(0, raw.shape[0], GROUP):
            for c in range(0, raw.shape[1], 2 * LANES):
                spot = (slice(r, r + GROUP), slice(c, c + 2 * LANES))
                hid[spot] = jax.nn.gelu(raw[spot]).astype(BF16)

    @pl.when(j == 0)
    def _():
        raw[...] = dot32(n_s[...], w1_ref[...])

    @pl.when((j > 0) & (j < n_tiles))
    def _():
        activate()
        raw[...] = dot32(n_s[...], w1_ref[...])
        acc[...] += dot32(hid[...], w2_ref[...])

    @pl.when(j == n_tiles)
    def _():
        activate()
        acc[...] += dot32(hid[...], w2_ref[...])
        finish()


def layers_kernel(n_tiles, own_ref, got_ref, w1_ref, w2_ref, o_ref, x_s, n_s, raw, hid, acc):
    layer, j = pl.program_id(0), pl.program_id(1)
    stage = lax.axis_index("pp")

    @pl.when((layer == 0) & (j == 0) & (stage == 0))
    def _():
        x_s[...] = own_ref[...]

    @pl.when((layer == 0) & (j == 0) & (stage != 0))
    def _():
        x_s[...] = got_ref[...]

    @pl.when(j == 0)
    def _():
        norm_rows(n_s, x_s)
        acc[...] = jnp.zeros_like(acc)

    def finish():
        for r in range(0, x_s.shape[0], GROUP):
            rs = slice(r, r + GROUP)
            out = (x_s[rs, :].astype(F32) + acc[rs, :]).astype(BF16)
            x_s[rs, :] = out
            o_ref[rs, :] = out

    ffn_steps(j, n_tiles, n_s, w1_ref, w2_ref, raw, hid, acc, finish)


def run_layers(own, own_block, got, rows, w_one, w_two):
    width = own.shape[1]
    _, n_layers, _, ffn = w_one.shape
    n_tiles = ffn // FFN_TILE
    whole = pl.BlockSpec((rows, width), lambda l, j: (0, 0))
    return pl.pallas_call(
        functools.partial(layers_kernel, n_tiles),
        out_shape=jax.ShapeDtypeStruct((rows, width), BF16),
        grid=(n_layers, n_tiles + 1),
        in_specs=[
            pl.BlockSpec((rows, width), lambda l, j: (own_block, 0)),
            whole,
            pl.BlockSpec((None, None, width, FFN_TILE), lambda l, j: (0, l, 0, jnp.minimum(j, n_tiles - 1))),
            pl.BlockSpec((None, None, FFN_TILE, width), lambda l, j: (0, l, jnp.maximum(j - 1, 0), 0)),
        ],
        out_specs=whole,
        scratch_shapes=[
            pltpu.VMEM((rows, width), BF16),
            pltpu.VMEM((rows, width), BF16),
            pltpu.VMEM((rows, FFN_TILE), F32),
            pltpu.VMEM((rows, FFN_TILE), BF16),
            pltpu.VMEM((rows, width), F32),
        ],
        compiler_params=pltpu.CompilerParams(dimension_semantics=("arbitrary", "arbitrary"), vmem_limit_bytes=VMEM_BYTES),
        cost_estimate=pl.CostEstimate(
            flops=4 * rows * width * ffn * n_layers, bytes_accessed=4 * width * ffn * n_layers, transcendentals=0
        ),
        name="layers",
    )(own, got, w_one, w_two)


def mtp_kernel(
    n_proj, n_tiles, h_ref, e_ref, gf_ref, gh_ref, ge_ref, gm_ref, wp_ref, w1_ref, w2_ref, o_ref,
    cat_s, z_s, n_s, raw, hid, acc,
):
    step = pl.program_id(0)
    rows, width = h_ref.shape
    proj_tile = wp_ref.shape[0]

    @pl.when(step == 0)
    def _():
        norm_rows(cat_s.at[:, pl.ds(0, width)], h_ref, gh_ref)
        norm_rows(cat_s.at[:, pl.ds(width, width)], e_ref, ge_ref)
        norm_rows(o_ref, h_ref, gf_ref)
        acc[...] = jnp.zeros_like(acc)

    @pl.when(step < n_proj)
    def _():
        at = pl.multiple_of(step * proj_tile, proj_tile)
        acc[...] += dot32(cat_s[:, pl.ds(at, proj_tile)], wp_ref[...])

    @pl.when(step == n_proj - 1)
    def _():
        for r in range(0, rows, GROUP):
            z_s[r:r + GROUP, :] = acc[r:r + GROUP, :].astype(BF16)
        norm_rows(n_s, z_s, gm_ref)
        acc[...] = jnp.zeros_like(acc)

    def finish():
        for r in range(0, rows, GROUP):
            rs = slice(r, r + GROUP)
            z_s[rs, :] = (z_s[rs, :].astype(F32) + acc[rs, :]).astype(BF16)
        norm_rows(o_ref, z_s, gf_ref, rows)

    ffn_steps(step - n_proj, n_tiles, n_s, w1_ref, w2_ref, raw, hid, acc, finish)


def run_mtp(h_last, e_rows, rows, gain_f, gain_h, gain_e, gain_m, w_proj, u_one, u_two):
    width = h_last.shape[1]
    ffn = u_one.shape[1]
    n_tiles = ffn // FFN_TILE
    n_proj = w_proj.shape[0] // FFN_TILE
    whole = pl.BlockSpec((rows, width), lambda s: (0, 0))
    gain = pl.BlockSpec((1, width), lambda s: (0, 0))
    return pl.pallas_call(
        functools.partial(mtp_kernel, n_proj, n_tiles),
        out_shape=jax.ShapeDtypeStruct((2 * rows, width), BF16),
        grid=(n_proj + n_tiles + 1,),
        in_specs=[
            whole, whole, gain, gain, gain, gain,
            pl.BlockSpec((FFN_TILE, width), lambda s: (jnp.minimum(s, n_proj - 1), 0)),
            pl.BlockSpec((width, FFN_TILE), lambda s: (0, jnp.clip(s - n_proj, 0, n_tiles - 1))),
            pl.BlockSpec((FFN_TILE, width), lambda s: (jnp.clip(s - n_proj - 1, 0, n_tiles - 1), 0)),
        ],
        out_specs=pl.BlockSpec((2 * rows, width), lambda s: (0, 0)),
        scratch_shapes=[
            pltpu.VMEM((rows, 2 * width), BF16),
            pltpu.VMEM((rows, width), BF16),
            pltpu.VMEM((rows, width), BF16),
            pltpu.VMEM((rows, FFN_TILE), F32),
            pltpu.VMEM((rows, FFN_TILE), BF16),
            pltpu.VMEM((rows, width), F32),
        ],
        compiler_params=pltpu.CompilerParams(dimension_semantics=("arbitrary",), vmem_limit_bytes=VMEM_BYTES),
        cost_estimate=pl.CostEstimate(
            flops=4 * rows * width * (ffn + width), bytes_accessed=4 * width * (ffn + width), transcendentals=0
        ),
        name="mtp",
    )(h_last, e_rows, gain_f[None], gain_h[None], gain_e[None], gain_m[None], w_proj, u_one, u_two)


def head_stats(buf, n_cols, base, tgt_ref, m_ref, s_ref, p_ref):
    rows = buf.shape[0]
    lane = lax.broadcasted_iota(jnp.int32, (GROUP, LANES), 1)
    for r in range(0, rows, GROUP):
        rs = slice(r, r + GROUP)
        parts = [buf[rs, c:c + LANES] for c in range(0, n_cols, LANES)]
        top = parts[0]
        for part in parts[1:]:
            top = jnp.maximum(top, part)
        m_old = m_ref[rs, :]
        m_new = jnp.maximum(m_old, top)
        total = s_ref[rs, :] * jnp.exp(m_old - m_new)
        rel = tgt_ref[rs, :] - lane - base
        pick = p_ref[rs, :]
        for k, part in enumerate(parts):
            total = total + jnp.exp(part - m_new)
            pick = jnp.where(rel == k * LANES, part, pick)
        m_ref[rs, :] = m_new
        s_ref[rs, :] = total
        p_ref[rs, :] = pick


def head_kernel(n_steps, tail, first, x_ref, tgt_ref, w_ref, o_ref, buf_a, buf_b, t_ref, m_ref, s_ref, p_ref):
    i = pl.program_id(0)
    half = buf_a.shape[1]
    rows = x_ref.shape[0] // 2
    n_seq = tgt_ref.shape[0] // 2
    state = (t_ref, m_ref, s_ref, p_ref)
    row = lax.broadcasted_iota(I32, (GROUP, LANES), 0)
    lane = lax.broadcasted_iota(I32, (GROUP, LANES), 1)

    @pl.when(i == 0)
    def _():
        buf_b[...] = jnp.full_like(buf_b, -3e38)
        m_ref[...] = jnp.full_like(m_ref, -3e38)
        s_ref[...] = jnp.zeros_like(s_ref)
        p_ref[...] = jnp.zeros_like(p_ref)
        for part in range(2):
            for r in range(0, rows, GROUP):
                want = jnp.zeros((GROUP, LANES), F32)
                for q in range(n_seq):
                    line = tgt_ref[part * n_seq + q:part * n_seq + q + 1, :].astype(F32)
                    want = want + jnp.where(q * LANES + lane == first + r + row, jnp.broadcast_to(line, want.shape), 0.0)
                want = jnp.sum(want, axis=1, keepdims=True)
                at = part * rows + r
                t_ref[at:at + GROUP, :] = jnp.broadcast_to(want, (GROUP, LANES)).astype(I32)

    @pl.when(i < n_steps - 1)
    def _():
        buf_a[...] = dot32(x_ref[...], w_ref[:, :half])
        head_stats(buf_b, half, (2 * i - 1) * half, *state)
        buf_b[...] = dot32(x_ref[...], w_ref[:, half:])
        head_stats(buf_a, half, 2 * i * half, *state)

    @pl.when(i == n_steps - 1)
    def _():
        head_stats(buf_b, half, (2 * i - 1) * half, *state)
        done = 0
        while done < tail:
            cols = min(half, tail - done)
            buf_a[:, :cols] = dot32(x_ref[...], w_ref[:, done:done + cols])
            head_stats(buf_a, cols, 2 * i * half + done, *state)
            done += cols
        for part in range(2):
            lines = [jnp.zeros((1, LANES), F32) for _ in range(n_seq)]
            for r in range(0, rows, GROUP):
                rs = slice(part * rows + r, part * rows + r + GROUP)
                top = jnp.max(m_ref[rs, :], axis=1, keepdims=True)
                total = jnp.sum(s_ref[rs, :] * jnp.exp(m_ref[rs, :] - top), axis=1, keepdims=True)
                picked = jnp.sum(p_ref[rs, :], axis=1, keepdims=True)
                nll = jnp.broadcast_to(top + jnp.log(total) - picked, (GROUP, LANES))
                for q in range(n_seq):
                    if q * LANES < first + r + GROUP and first + r < (q + 1) * LANES:
                        here = jnp.where(q * LANES + lane == first + r + row, nll, 0.0)
                        lines[q] = lines[q] + jnp.sum(here, axis=0, keepdims=True)
            o_ref[part * n_seq:(part + 1) * n_seq, :] = jnp.concatenate(lines, axis=0)


def run_head(x_val, tgt_tile, first, w_out):
    rows, width = x_val.shape
    vocab = w_out.shape[1]
    tile = 2 * HEAD_HALF
    n_steps = pl.cdiv(vocab, tile)
    tail = vocab - (n_steps - 1) * tile
    small = pl.BlockSpec(tgt_tile.shape, lambda i: (0, 0))
    return pl.pallas_call(
        functools.partial(head_kernel, n_steps, tail, first),
        out_shape=jax.ShapeDtypeStruct(tgt_tile.shape, F32),
        grid=(n_steps,),
        in_specs=[
            pl.BlockSpec((rows, width), lambda i: (0, 0)),
            small,
            pl.BlockSpec((width, tile), lambda i: (0, i)),
        ],
        out_specs=small,
        scratch_shapes=[pltpu.VMEM((rows, HEAD_HALF), F32)] * 2
        + [pltpu.VMEM((rows, LANES), I32)]
        + [pltpu.VMEM((rows, LANES), F32)] * 3,
        compiler_params=pltpu.CompilerParams(dimension_semantics=("arbitrary",), vmem_limit_bytes=VMEM_BYTES),
        cost_estimate=pl.CostEstimate(flops=2 * rows * width * vocab, bytes_accessed=2 * width * vocab, transcendentals=0),
        name="head",
    )(x_val, tgt_tile, w_out)


def solution(mesh):
    n_data = mesh.shape["dp"]
    n_stages = mesh.shape["pp"]

    def extra_rows(table, want, j):
        me = lax.axis_index("dp")
        n_local = table.shape[0]
        ids_all = lax.all_gather(want, "dp")
        held = ids_all // n_local == me
        rank = jnp.cumsum(held.astype(I32), axis=1) - 1
        slot = j * CAP + jnp.arange(CAP)
        hit = held[:, None, :] & (rank[:, None, :] == slot[None, :, None])
        idx = jnp.sum(jnp.where(hit, (ids_all - me * n_local)[:, None, :], 0), axis=2)
        packed = table[idx]
        got = lax.all_to_all(packed, "dp", 0, 0)
        owner = want // n_local
        mine = owner[:, None] == jnp.arange(n_data)[None, :]
        ranks = jnp.sum(jnp.where(mine, jnp.cumsum(mine.astype(I32), axis=0) - 1, 0), axis=1) - j * CAP
        place = jnp.where((ranks >= 0) & (ranks < CAP), owner * CAP + ranks, -1)
        pick = (place[:, None] == jnp.arange(n_data * CAP)[None, :]).astype(BF16)
        return dot32(pick, got.reshape(n_data * CAP, -1)).astype(BF16)

    def body(tok_ids, emb_s, w_one, w_two, gain_f, gain_h, gain_e, gain_m, w_proj, u_one, u_two, w_out):
        stage = lax.axis_index("pp")
        n_micro, batch_dev, seq_plus = tok_ids.shape
        seq_len = seq_plus - 2
        n_seq = n_micro * batch_dev
        n_tok = n_seq * seq_len
        assert seq_len == LANES and 2 * n_seq == BLOCK
        rows_a = ROWS_A
        rows_b = n_tok - rows_a
        table = emb_s[0]
        n_local = table.shape[0]
        ids = tok_ids.reshape(n_seq, seq_plus)
        spare = jnp.full((n_seq, seq_len - 1), -1, I32)
        ids_tile = jnp.concatenate([ids[:, :seq_len + 1], spare], axis=1).reshape(2 * n_seq, seq_len)
        tgt_tile = jnp.concatenate([ids[:, 1:seq_len + 1], ids[:, 2:]], axis=0)

        idx, most = run_slots(ids_tile, n_data, n_local)
        packed = run_pack(idx, table)
        x_all, e_all = run_trade(ids_tile, packed, n_local, n_seq, 2 * rows_a)

        def more(carry):
            j, x_val, e_val = carry
            rows = extra_rows(table, ids[:, :seq_len + 1].reshape(-1), j).reshape(n_seq, seq_len + 1, -1)
            x_more = rows[:, :seq_len].reshape(n_tok, -1)
            e_more = rows[:, 1:].reshape(n_tok, -1)
            return j + 1, x_val + jnp.pad(x_more, ((0, 2 * rows_a - n_tok), (0, 0))), e_val + e_more

        most = most[0, 0]
        _, x_all, e_all = lax.while_loop(lambda c: c[0] * CAP < most, more, (jnp.int32(1), x_all, e_all))

        x_mid = run_layers(x_all, 0, x_all, rows_a, w_one, w_two)
        moved, e_last = run_hand_on(x_mid, e_all)
        swapped = run_swap(run_layers(x_all, 1, moved, rows_a, w_one, w_two))

        def tail(h_last, e_rows, first, rows):
            normed = run_mtp(h_last, e_rows, rows, gain_f, gain_h, gain_e, gain_m, w_proj, u_one, u_two)
            return run_head(normed, tgt_tile, first, w_out)

        def tail_first():
            return tail(swapped, e_all, 0, rows_a)

        def tail_last():
            return tail(run_layers(swapped, 0, swapped, rows_b, w_one, w_two), e_last, rows_a, rows_b)

        tile = lax.cond(stage == 0, tail_first, tail_last)
        nll, total = run_finish(tile, n_data, n_stages, 1.0 / (n_tok * n_data))
        shape = (n_micro, batch_dev, seq_len)
        return total[0, 0], nll[:n_seq].reshape(shape), nll[n_seq:].reshape(shape)

    rep = P()
    in_specs = (P(None, "dp", None), P("pp", "dp", None), P("pp"), P("pp")) + (rep,) * 8
    out_specs = (rep, P(None, "dp", None), P(None, "dp", None))
    return jax.shard_map(body, mesh=mesh, in_specs=in_specs, out_specs=out_specs, check_vma=False)
```

time: 561 us -> 496 us (0.88)
  Pallas kernels: 394 us -> 460 us
  local copies, waits for them, and re-layouts: 54.2 us -> 7.6 us
  blocking collectives: 37 us -> 0 us
  starting transfers between devices: 28.5 us -> 0 us
  other arithmetic: 12.7 us -> 0.02 us
  loops' own time: 11.5 us -> 19.3 us
    pallas_call x1 -> x7, Pallas kernels: 236 us -> 304 us  [the longest x1 236 us: run_head(): pl.pallas_call(functools.partial(head_kernel, n_steps, tail, first), out_...]
    gather x17 -> x0, local copies, waits for them, and re-layouts: 38.6 us -> none  [the longest x8 34.8 us: one_round(): packed = [table[idx[k]] for k in range(n_data)]]
    ppermute x9 -> x0, starting transfers between devices: 28.5 us -> none  [the longest x6 20.4 us: one_round(): lax.ppermute(packed[k], ('dp', 'pp'), swap_perm(k))]
    psum x2 -> x0, blocking collectives: 27 us -> none  [the longest x1 23.8 us: body(): total_loss = lax.psum(local_sum, ('dp', 'pp')) / (n_tok * n_data)]
    all_gather x1 -> x0, blocking collectives: 10 us -> none  [body(): ids_all = lax.all_gather(want, 'dp')]
    another operation x3 -> x2, loops' own time: 11.5 us -> 19.3 us  [the longest x1 18.7 us: body(): lax.while_loop(lambda c: c[0] * CAP < most, more, (jnp.int32(1), x_all, e...]
  transfers between devices with their start and end apart: 9 -> 0, of which waited for: 1 -> 0; matrix products, arithmetic and copies ran while one was open for 9% -> 0% of each run, Pallas kernels for 11% -> 0%
where the time goes in v2:
time: 496 us; the launch traced here: 488 us
  Pallas kernels  460 us (93%)
  loops' own time  19.3 us (4%)
  local copies, waits for them, and re-layouts  7.6 us (2%)
    pallas_call x1, Pallas kernels, run_head(): pl.pallas_call(functools.partial(head_kernel, n_steps, tail, first), out_...  236 us
    pallas_call x2, Pallas kernels, run_layers(): pl.pallas_call(functools.partial(layers_kernel, n_tiles), out_shape=jax.S...  116 us
    pallas_call x1, Pallas kernels, run_mtp(): pl.pallas_call(functools.partial(mtp_kernel, n_proj, n_tiles), out_shape=...  40.5 us
    pallas_call x1, Pallas kernels, run_trade(): pl.pallas_call(functools.partial(trade_kernel, n_data, n_local, n_seq), o...  27.3 us
    another operation x1, loops' own time, body(): lax.while_loop(lambda c: c[0] * CAP < most, more, (jnp.int32(1), x_all, e...  18.7 us
    pallas_call x1, Pallas kernels, run_pack(): pl.pallas_call(functools.partial(pack_kernel, n_data), out_shape=jax.Shap...  15.7 us

profile of v2, /device:TPU:0, one launch (start us, length us, event | category | flops | bytes accessed | tf_op | source)
XLA Modules:
  0.0 488.3 jit_solution(4276481513928197692)
XLA Ops:
  0.6 0.7 reshape.204
  1.3 0.6 reshape.205.ids_ref
  1.9 9.0 %slots.1 = (s32[4,256]{1,0:T(4,128)}, s32[8,128]{1,0:T(8,128)}) custom-call(s32[8,128]{1,0:T(8,128)} %reshape.205.ids_ref), custom_call_target="tpu_custom_call" | custom-call | tf_op jit(solution)/shard_map/slots/pallas_call | solution.py:112
  10.9 15.7 %pack.1.packed_ref = bf16[4,176,2048]{2,1,0:T(8,128)(2,1)} custom-call(s32[4,256]{1,0:T(4,128)} %get-tuple-element.205.idx_ref.lane_ref, s32[4,256]{1,0:T(4,128)} %get-tuple-element.205.idx_ref.lane_ref, bf16[23136,2048]{1,0:T(8,128)(2,1)} %bitcast.8.table_ref), custom_call_target="tpu_custom_call" | custom-call | tf_op jit(solution)/shard_map/pack/pallas_call | solution.py:164
  26.7 27.3 %trade.1 = (bf16[576,2048]{1,0:T(8,128)(2,1)}, bf16[512,2048]{1,0:T(8,128)(2,1)}) custom-call(s32[8,128]{1,0:T(8,128)} %reshape.205.ids_ref, bf16[4,176,2048]{2,1,0:T(8,128)(2,1)} %pack.1.packed_ref), custom_call_target="tpu_custom_call" | custom-call | tf_op jit(solution)/shard_map/trade/pallas_call | solution.py:235
  54.0 1.2 slice.86
  55.2 0.1 sign.34
  55.3 18.7 %while.15 = (s32[]{:T(128)}, bf16[576,2048]{1,0:T(8,128)(2,1)}, bf16[512,2048]{1,0:T(8,128)(2,1)}, s32[]{:T(128)}, s32[516,1]{0,1:T(1,128)S(1)}, /*index=5*/s32[...) while((s32[]{:T(128)}, bf16[576,2048]{1,0:T(8,128)(2,1)}, ...), condition=%wide.region_7.8_spmd, body=%wide.region_0.7_spmd.sunk | while | flops 1497272576 | bytes 81143688 | solution.py:658
  74.0 0.0 copy-start.2
  74.0 58.4 %layers.4.x_ref = bf16[288,2048]{1,0:T(8,128)(2,1)} custom-call(bf16[576,2048]{1,0:T(8,128)(2,1)} %get-tuple-element.209.own_ref.got_ref, bf16[576,2048]{1,0:T(8,128)(2,1)} %get-tuple-element.209.own_ref.got_ref, bf16[1,2,2048,8192]{3,2,1,0:T(8,128)(2,1)} %w1_ref.3, bf16[1,2,8192,2048]{3,2,1,0:T(8,128)(2,1)} %w2_ref.3), custom_call_target="tpu_custom_call" | custom-call | flops 38654705664 | bytes 134217728 | tf_op jit(solution)/shard_map/layers/pallas_call | solution.py:408
  132.4 0.0 copy-done.2
  132.4 3.8 hand_on.1
  136.2 57.3 %layers.5.x_ref = bf16[288,2048]{1,0:T(8,128)(2,1)} custom-call(bf16[576,2048]{1,0:T(8,128)(2,1)} %get-tuple-element.209.own_ref.got_ref, bf16[288,2048]{1,0:T(8,128)(2,1)} %get-tuple-element.211.got_ref, bf16[1,2,2048,8192]{3,2,1,0:T(8,128)(2,1)} %w1_ref.3, bf16[1,2,8192,2048]{3,2,1,0:T(8,128)(2,1)} %w2_ref.3), custom_call_target="tpu_custom_call" | custom-call | flops 38654705664 | bytes 134217728 | tf_op jit(solution)/shard_map/layers/pallas_call | solution.py:408
  193.5 0.0 copy-start.3
  193.5 0.0 copy-start.7
  193.5 0.0 copy-start.8
  193.5 0.0 copy-start.9
  193.5 0.0 copy-start.10
  193.5 2.9 swap.1
  196.4 0.1 fusion.7
  196.5 0.0 copy-done.3
  196.5 0.0 copy-done.7
  196.5 0.0 copy-done.8
  196.5 0.0 copy-done.9
  196.5 0.0 copy-done.10
  196.5 279.2 %conditional.1 = (f32[8,128]{1,0:T(8,128)S(1)}) conditional(s32[]{:T(128)} %convert_element_type.26, (bf16[288,2048]{1,0:T(8,128)(2,1)S(1)}, bf16[1,2,2048,8192]{3,2,1,0:T(8,128)(2,1)}, bf16[1,2,8192,2048]{3,2,1,0:T(8,128)(2,1)}, bf16[2048]{0:T(1024)(128)(2,1)S(1)}, bf16[2048]{0:T(1024)(128)(2,1)S(1)}, /*index=5*/bf16[2048]{0:T(1024)(128)(2,1)S(1)}, ...), branch_computations={%region_8.9_spmd, %region_9.10_spmd} | conditional | flops 242497880064 | bytes 600866816 | solution.py:674
  196.9 0.6 broadcast_in_dim.60.gf_ref
  197.5 0.6 broadcast_in_dim.61.gh_ref
  198.1 0.6 broadcast_in_dim.62.ge_ref
  198.7 0.6 broadcast_in_dim.63.gm_ref
  199.3 40.5 %mtp.3.x_ref = bf16[576,2048]{1,0:T(8,128)(2,1)} custom-call(bf16[288,2048]{1,0:T(8,128)(2,1)S(1)} %get-tuple-element.181.h_ref, bf16[512,2048]{1,0:T(8,128)(2,1)S(1)} %get-tuple-element.182.e_ref, bf16[1,2048]{1,0:T(2,128)(2,1)} %broadcast_in_dim.60.gf_ref, bf16[1,2048]{1,0:T(2,128)(2,1)} %broadcast_in_dim.61.gh_ref, ...), custom_call_target="tpu_custom_call" | custom-call | flops 24159191040 | bytes 83886080 | tf_op jit(solution)/shard_map/cond/branch_1_fun/mtp/pallas_call | solution.py:477
  239.8 235.7 %head.3 = f32[8,128]{1,0:T(8,128)S(1)} custom-call(bf16[576,2048]{1,0:T(8,128)(2,1)} %mtp.3.x_ref, s32[8,128]{1,0:T(8,128)S(1)} %get-tuple-element.190.tgt_ref, bf16[2048,92544]{1,0:T(8,128)(2,1)} %get-tuple-element.191.w_ref), custom_call_target="tpu_custom_call" | custom-call | flops 218338689024 | bytes 379060224 | tf_op jit(solution)/shard_map/cond/branch_1_fun/head/pallas_call | solution.py:589
  475.7 9.8 %finish.1 = (f32[8,128]{1,0:T(8,128)}, f32[8,128]{1,0:T(8,128)}) custom-call(f32[8,128]{1,0:T(8,128)S(1)} %get-tuple-element.330.x_ref), custom_call_target="tpu_custom_call" | custom-call | tf_op jit(solution)/shard_map/finish/pallas_call | solution.py:337
  485.6 1.3 fusion.6
  486.9 1.2 slice.89
  (3 shorter events, 0.0 us)
Async XLA Ops:
  74.0 58.4 %copy-start.2 = (bf16[512,2048]{1,0:T(8,128)(2,1)S(1)}, bf16[512,2048]{1,0:T(8,128)(2,1)}, u32[]{:S(2)}) copy-start(bf16[512,2048]{1,0:T(8,128)(2,1)} %get-tuple-element.210.e_ref) | copy-start | bytes 6291460
  193.5 3.0 copy-start.3
  193.5 3.0 copy-start.7
  193.5 3.0 copy-start.8
  193.5 3.0 copy-start.9
  193.5 3.0 copy-start.10

commit v3 on v2

--- a/solution.py
+++ b/solution.py
@@ -20,7 +20,9 @@
 ROWS_A = 288
 FFN_TILE = 1024
 HEAD_HALF = 1024
-CAP = 176
+HEAD_PARTS = 4
+CAP = 160
+SLOTS = 3
 BLOCK = 8
 
 
@@ -73,7 +75,7 @@
     return jnp.concatenate(out, axis=0)
 
 
-def slots_kernel(n_data, n_local, ids_ref, idx_ref, most_ref, got, send_sem, recv_sem):
+def slots_kernel(n_data, n_local, ids_ref, idx_ref, most_ref, all_ref, got, send_sem, recv_sem):
     me, stage = lax.axis_index("dp"), lax.axis_index("pp")
     peers = [(jnp.bitwise_xor(me, k), stage) for k in range(1, n_data)]
     enter(peers)
@@ -86,6 +88,7 @@
     slot = lax.broadcasted_iota(I32, (CAP, LANES), 0).astype(F32)
     for k in range(n_data):
         ids = ids_ref[...] if k == 0 else got[k - 1]
+        all_ref[k] = ids
         for s in range(n_data):
             inside = ((ids >= s * n_local) & (ids < (s + 1) * n_local)).astype(F32)
             most = jnp.maximum(most, jnp.sum(jnp.sum(inside, axis=1, keepdims=True), axis=0, keepdims=True))
@@ -111,9 +114,10 @@
     vmem = pl.BlockSpec(memory_space=pltpu.VMEM)
     return pl.pallas_call(
         functools.partial(slots_kernel, n_data, n_local),
-        out_shape=[jax.ShapeDtypeStruct((n_data, 2 * LANES), I32), jax.ShapeDtypeStruct((BLOCK, LANES), I32)],
+        out_shape=[jax.ShapeDtypeStruct((n_data, 2 * LANES), I32), jax.ShapeDtypeStruct((BLOCK, LANES), I32),
+                   jax.ShapeDtypeStruct((n_data, BLOCK, LANES), I32)],
         in_specs=[vmem],
-        out_specs=[vmem, vmem],
+        out_specs=[vmem, vmem, vmem],
         scratch_shapes=[
             pltpu.VMEM((n_data - 1, BLOCK, LANES), I32),
             pltpu.SemaphoreType.DMA((n_data - 1,)),
@@ -218,7 +222,7 @@
         first = placed(0, packed_ref[0])
         x_ref[:n_tok, :] = first[:n_tok]
         e_ref[:n_tok, :] = first[n_tok:]
-        for k in range(n_data - 1):
+        for k in (2, 0, 1):
             copies[k].wait()
             add(placed(k + 1, got[k]))
 
@@ -349,7 +353,12 @@
     )(tile)
 
 
-def ffn_steps(j, n_tiles, n_s, w1_ref, w2_ref, raw, hid, acc, finish):
+def ring_copy(src, ring, sems, i):
+    slot = lax.rem(i, SLOTS)
+    return pltpu.make_async_copy(src, ring.at[slot], sems.at[slot])
+
+
+def ffn_steps(j, n_tiles, n_s, w1_slot, w2_slot, ring1, ring2, raw, hid, acc, finish):
     def activate():
         for r in range(0, raw.shape[0], GROUP):
             for c in range(0, raw.shape[1], 2 * LANES):
@@ -358,30 +367,46 @@
 
     @pl.when(j == 0)
     def _():
-        raw[...] = dot32(n_s[...], w1_ref[...])
+        raw[...] = dot32(n_s[...], ring1[w1_slot])
 
     @pl.when((j > 0) & (j < n_tiles))
     def _():
         activate()
-        raw[...] = dot32(n_s[...], w1_ref[...])
-        acc[...] += dot32(hid[...], w2_ref[...])
+        raw[...] = dot32(n_s[...], ring1[w1_slot])
+        acc[...] += dot32(hid[...], ring2[w2_slot])
 
     @pl.when(j == n_tiles)
     def _():
         activate()
-        acc[...] += dot32(hid[...], w2_ref[...])
+        acc[...] += dot32(hid[...], ring2[w2_slot])
         finish()
 
 
-def layers_kernel(n_tiles, own_ref, got_ref, w1_ref, w2_ref, o_ref, x_s, n_s, raw, hid, acc):
+def layers_kernel(n_tiles, n_layers, own_ref, got_ref, w1_hbm, w2_hbm, o_ref, x_s, n_s, raw, hid, acc, ring1, ring2, sem1, sem2):
     layer, j = pl.program_id(0), pl.program_id(1)
     stage = lax.axis_index("pp")
-
-    @pl.when((layer == 0) & (j == 0) & (stage == 0))
+    total = n_layers * n_tiles
+    up, down = layer * n_tiles + j, layer * n_tiles + j - 1
+
+    def copy1(i):
+        col = pl.multiple_of(lax.rem(i, n_tiles) * FFN_TILE, FFN_TILE)
+        return ring_copy(w1_hbm.at[0, lax.div(i, n_tiles), :, pl.ds(col, FFN_TILE)], ring1, sem1, i)
+
+    def copy2(i):
+        row = pl.multiple_of(lax.rem(i, n_tiles) * FFN_TILE, FFN_TILE)
+        return ring_copy(w2_hbm.at[0, lax.div(i, n_tiles), pl.ds(row, FFN_TILE), :], ring2, sem2, i)
+
+    start = (layer == 0) & (j == 0)
+
+    @pl.when(start)
+    def _():
+        copy1(0).start()
+
+    @pl.when(start & (stage == 0))
     def _():
         x_s[...] = own_ref[...]
 
-    @pl.when((layer == 0) & (j == 0) & (stage != 0))
+    @pl.when(start & (stage != 0))
     def _():
         x_s[...] = got_ref[...]
 
@@ -389,6 +414,28 @@
     def _():
         norm_rows(n_s, x_s)
         acc[...] = jnp.zeros_like(acc)
+
+    @pl.when(start)
+    def _():
+        copy1(1).start()
+        copy2(0).start()
+        copy2(1).start()
+
+    @pl.when(j < n_tiles)
+    def _():
+        copy1(up).wait()
+
+        @pl.when(up + SLOTS - 1 < total)
+        def _():
+            copy1(up + SLOTS - 1).start()
+
+    @pl.when(j > 0)
+    def _():
+        copy2(down).wait()
+
+        @pl.when(down + SLOTS - 1 < total)
+        def _():
+            copy2(down + SLOTS - 1).start()
 
     def finish():
         for r in range(0, x_s.shape[0], GROUP):
@@ -397,7 +444,18 @@
             x_s[rs, :] = out
             o_ref[rs, :] = out
 
-    ffn_steps(j, n_tiles, n_s, w1_ref, w2_ref, raw, hid, acc, finish)
+    ffn_steps(
+        j, n_tiles, n_s, lax.rem(up, SLOTS), lax.rem(jnp.maximum(down, 0), SLOTS), ring1, ring2, raw, hid, acc, finish
+    )
+
+
+def ring_scratch(width):
+    return [
+        pltpu.VMEM((SLOTS, width, FFN_TILE), BF16),
+        pltpu.VMEM((SLOTS, FFN_TILE, width), BF16),
+        pltpu.SemaphoreType.DMA((SLOTS,)),
+        pltpu.SemaphoreType.DMA((SLOTS,)),
+    ]
 
 
 def run_layers(own, own_block, got, rows, w_one, w_two):
@@ -405,16 +463,12 @@
     _, n_layers, _, ffn = w_one.shape
     n_tiles = ffn // FFN_TILE
     whole = pl.BlockSpec((rows, width), lambda l, j: (0, 0))
-    return pl.pallas_call(
-        functools.partial(layers_kernel, n_tiles),
+    hbm = pl.BlockSpec(memory_space=pl.ANY)
+    return pl.pallas_call(
+        functools.partial(layers_kernel, n_tiles, n_layers),
         out_shape=jax.ShapeDtypeStruct((rows, width), BF16),
         grid=(n_layers, n_tiles + 1),
-        in_specs=[
-            pl.BlockSpec((rows, width), lambda l, j: (own_block, 0)),
-            whole,
-            pl.BlockSpec((None, None, width, FFN_TILE), lambda l, j: (0, l, 0, jnp.minimum(j, n_tiles - 1))),
-            pl.BlockSpec((None, None, FFN_TILE, width), lambda l, j: (0, l, jnp.maximum(j - 1, 0), 0)),
-        ],
+        in_specs=[pl.BlockSpec((rows, width), lambda l, j: (own_block, 0)), whole, hbm, hbm],
         out_specs=whole,
         scratch_shapes=[
             pltpu.VMEM((rows, width), BF16),
@@ -422,7 +476,7 @@
             pltpu.VMEM((rows, FFN_TILE), F32),
             pltpu.VMEM((rows, FFN_TILE), BF16),
             pltpu.VMEM((rows, width), F32),
-        ],
+        ] + ring_scratch(width),
         compiler_params=pltpu.CompilerParams(dimension_semantics=("arbitrary", "arbitrary"), vmem_limit_bytes=VMEM_BYTES),
         cost_estimate=pl.CostEstimate(
             flops=4 * rows * width * ffn * n_layers, bytes_accessed=4 * width * ffn * n_layers, transcendentals=0
@@ -432,24 +486,63 @@
 
 
 def mtp_kernel(
-    n_proj, n_tiles, h_ref, e_ref, gf_ref, gh_ref, ge_ref, gm_ref, wp_ref, w1_ref, w2_ref, o_ref,
-    cat_s, z_s, n_s, raw, hid, acc,
+    n_proj, n_tiles, h_ref, e_ref, gf_ref, gh_ref, ge_ref, gm_ref, wp_hbm, w1_hbm, w2_hbm, o_ref,
+    cat_s, z_s, n_s, raw, hid, acc, ring1, ring2, sem1, sem2,
 ):
     step = pl.program_id(0)
     rows, width = h_ref.shape
-    proj_tile = wp_ref.shape[0]
+    j = step - n_proj
+    total2 = n_proj + n_tiles
+    second = jnp.where(step < n_proj, step, step - 1)
+
+    def copy1(i):
+        col = pl.multiple_of(i * FFN_TILE, FFN_TILE)
+        return ring_copy(w1_hbm.at[:, pl.ds(col, FFN_TILE)], ring1, sem1, i)
+
+    def copy2(src, i, tile):
+        row = pl.multiple_of(tile * FFN_TILE, FFN_TILE)
+        return ring_copy(src.at[pl.ds(row, FFN_TILE), :], ring2, sem2, i)
+
+    def feed2(i):
+        @pl.when(i < n_proj)
+        def _():
+            copy2(wp_hbm, i, i).start()
+
+        @pl.when((i >= n_proj) & (i < total2))
+        def _():
+            copy2(w2_hbm, i, i - n_proj).start()
 
     @pl.when(step == 0)
     def _():
+        copy2(wp_hbm, 0, 0).start()
         norm_rows(cat_s.at[:, pl.ds(0, width)], h_ref, gh_ref)
         norm_rows(cat_s.at[:, pl.ds(width, width)], e_ref, ge_ref)
         norm_rows(o_ref, h_ref, gf_ref)
         acc[...] = jnp.zeros_like(acc)
+        copy2(wp_hbm, 1, 1).start()
+
+    @pl.when(step == n_proj - 2)
+    def _():
+        copy1(0).start()
+        copy1(1).start()
+
+    @pl.when(j != 0)
+    def _():
+        copy2(wp_hbm, second, 0).wait()
+        feed2(second + SLOTS - 1)
+
+    @pl.when((j >= 0) & (j < n_tiles))
+    def _():
+        copy1(j).wait()
+
+        @pl.when(j + SLOTS - 1 < n_tiles)
+        def _():
+            copy1(j + SLOTS - 1).start()
 
     @pl.when(step < n_proj)
     def _():
-        at = pl.multiple_of(step * proj_tile, proj_tile)
-        acc[...] += dot32(cat_s[:, pl.ds(at, proj_tile)], wp_ref[...])
+        at = pl.multiple_of(step * FFN_TILE, FFN_TILE)
+        acc[...] += dot32(cat_s[:, pl.ds(at, FFN_TILE)], ring2[lax.rem(second, SLOTS)])
 
     @pl.when(step == n_proj - 1)
     def _():
@@ -464,7 +557,9 @@
             z_s[rs, :] = (z_s[rs, :].astype(F32) + acc[rs, :]).astype(BF16)
         norm_rows(o_ref, z_s, gf_ref, rows)
 
-    ffn_steps(step - n_proj, n_tiles, n_s, w1_ref, w2_ref, raw, hid, acc, finish)
+    ffn_steps(
+        j, n_tiles, n_s, lax.rem(jnp.maximum(j, 0), SLOTS), lax.rem(second, SLOTS), ring1, ring2, raw, hid, acc, finish
+    )
 
 
 def run_mtp(h_last, e_rows, rows, gain_f, gain_h, gain_e, gain_m, w_proj, u_one, u_two):
@@ -480,9 +575,7 @@
         grid=(n_proj + n_tiles + 1,),
         in_specs=[
             whole, whole, gain, gain, gain, gain,
-            pl.BlockSpec((FFN_TILE, width), lambda s: (jnp.minimum(s, n_proj - 1), 0)),
-            pl.BlockSpec((width, FFN_TILE), lambda s: (0, jnp.clip(s - n_proj, 0, n_tiles - 1))),
-            pl.BlockSpec((FFN_TILE, width), lambda s: (jnp.clip(s - n_proj - 1, 0, n_tiles - 1), 0)),
+            pl.BlockSpec(memory_space=pl.ANY), pl.BlockSpec(memory_space=pl.ANY), pl.BlockSpec(memory_space=pl.ANY),
         ],
         out_specs=pl.BlockSpec((2 * rows, width), lambda s: (0, 0)),
         scratch_shapes=[
@@ -492,7 +585,7 @@
             pltpu.VMEM((rows, FFN_TILE), F32),
             pltpu.VMEM((rows, FFN_TILE), BF16),
             pltpu.VMEM((rows, width), F32),
-        ],
+        ] + ring_scratch(width),
         compiler_params=pltpu.CompilerParams(dimension_semantics=("arbitrary",), vmem_limit_bytes=VMEM_BYTES),
         cost_estimate=pl.CostEstimate(
             flops=4 * rows * width * (ffn + width), bytes_accessed=4 * width * (ffn + width), transcendentals=0
@@ -550,19 +643,19 @@
 
     @pl.when(i < n_steps - 1)
     def _():
-        buf_a[...] = dot32(x_ref[...], w_ref[:, :half])
-        head_stats(buf_b, half, (2 * i - 1) * half, *state)
-        buf_b[...] = dot32(x_ref[...], w_ref[:, half:])
-        head_stats(buf_a, half, 2 * i * half, *state)
+        bufs = (buf_a, buf_b)
+        for q in range(HEAD_PARTS):
+            bufs[q % 2][...] = dot32(x_ref[...], w_ref[:, q * half:(q + 1) * half])
+            head_stats(bufs[(q + 1) % 2], half, (HEAD_PARTS * i + q - 1) * half, *state)
 
     @pl.when(i == n_steps - 1)
     def _():
-        head_stats(buf_b, half, (2 * i - 1) * half, *state)
+        head_stats(buf_b, half, (HEAD_PARTS * i - 1) * half, *state)
         done = 0
         while done < tail:
             cols = min(half, tail - done)
             buf_a[:, :cols] = dot32(x_ref[...], w_ref[:, done:done + cols])
-            head_stats(buf_a, cols, 2 * i * half + done, *state)
+            head_stats(buf_a, cols, HEAD_PARTS * i * half + done, *state)
             done += cols
         for part in range(2):
             lines = [jnp.zeros((1, LANES), F32) for _ in range(n_seq)]
@@ -582,7 +675,7 @@
 def run_head(x_val, tgt_tile, first, w_out):
     rows, width = x_val.shape
     vocab = w_out.shape[1]
-    tile = 2 * HEAD_HALF
+    tile = HEAD_PARTS * HEAD_HALF
     n_steps = pl.cdiv(vocab, tile)
     tail = vocab - (n_steps - 1) * tile
     small = pl.BlockSpec(tgt_tile.shape, lambda i: (0, 0))
@@ -609,23 +702,30 @@
     n_data = mesh.shape["dp"]
     n_stages = mesh.shape["pp"]
 
-    def extra_rows(table, want, j):
+    def swap_perm(k):
+        return [(d * n_stages, (d ^ k) * n_stages) for d in range(n_data)]
+
+    def extra_rows(table, ids_all, j):
         me = lax.axis_index("dp")
         n_local = table.shape[0]
-        ids_all = lax.all_gather(want, "dp")
-        held = ids_all // n_local == me
-        rank = jnp.cumsum(held.astype(I32), axis=1) - 1
-        slot = j * CAP + jnp.arange(CAP)
-        hit = held[:, None, :] & (rank[:, None, :] == slot[None, :, None])
+        ids_all = jnp.where(j > 0, ids_all, 0)
+        n = ids_all.shape[1]
+        before = (jnp.arange(n)[:, None] < jnp.arange(n)[None, :]).astype(BF16)
+        owner = ids_all // n_local
+
+        def ranks(held):
+            return dot32(held.astype(BF16), before).astype(I32) - j * CAP
+
+        held = owner == me
+        hit = held[:, None, :] & (ranks(held)[:, None, :] == jnp.arange(CAP)[None, :, None])
         idx = jnp.sum(jnp.where(hit, (ids_all - me * n_local)[:, None, :], 0), axis=2)
-        packed = table[idx]
-        got = lax.all_to_all(packed, "dp", 0, 0)
-        owner = want // n_local
-        mine = owner[:, None] == jnp.arange(n_data)[None, :]
-        ranks = jnp.sum(jnp.where(mine, jnp.cumsum(mine.astype(I32), axis=0) - 1, 0), axis=1) - j * CAP
-        place = jnp.where((ranks >= 0) & (ranks < CAP), owner * CAP + ranks, -1)
+        got = [table[idx[0]]] + [lax.ppermute(table[idx[k]], ("dp", "pp"), swap_perm(k)) for k in range(1, n_data)]
+        src = jnp.bitwise_xor(owner[0], me)
+        mine = src[None, :] == jnp.arange(n_data)[:, None]
+        rank = jnp.sum(jnp.where(mine, ranks(mine), 0), axis=0)
+        place = jnp.where((rank >= 0) & (rank < CAP), src * CAP + rank, -1)
         pick = (place[:, None] == jnp.arange(n_data * CAP)[None, :]).astype(BF16)
-        return dot32(pick, got.reshape(n_data * CAP, -1)).astype(BF16)
+        return dot32(pick, jnp.concatenate(got, axis=0)).astype(BF16)
 
     def body(tok_ids, emb_s, w_one, w_two, gain_f, gain_h, gain_e, gain_m, w_proj, u_one, u_two, w_out):
         stage = lax.axis_index("pp")
@@ -643,13 +743,14 @@
         ids_tile = jnp.concatenate([ids[:, :seq_len + 1], spare], axis=1).reshape(2 * n_seq, seq_len)
         tgt_tile = jnp.concatenate([ids[:, 1:seq_len + 1], ids[:, 2:]], axis=0)
 
-        idx, most = run_slots(ids_tile, n_data, n_local)
+        idx, most, ids_seen = run_slots(ids_tile, n_data, n_local)
         packed = run_pack(idx, table)
         x_all, e_all = run_trade(ids_tile, packed, n_local, n_seq, 2 * rows_a)
 
         def more(carry):
             j, x_val, e_val = carry
-            rows = extra_rows(table, ids[:, :seq_len + 1].reshape(-1), j).reshape(n_seq, seq_len + 1, -1)
+            wanted = ids_seen.reshape(n_data, n_seq, 2 * seq_len)[:, :, :seq_len + 1].reshape(n_data, -1)
+            rows = extra_rows(table, wanted, j).reshape(n_seq, seq_len + 1, -1)
             x_more = rows[:, :seq_len].reshape(n_tok, -1)
             e_more = rows[:, 1:].reshape(n_tok, -1)
             return j + 1, x_val + jnp.pad(x_more, ((0, 2 * rows_a - n_tok), (0, 0))), e_val + e_more

time: 496 us -> 461 us (0.929)
  Pallas kernels: 460 us -> 429 us
    pallas_call x2, Pallas kernels: 116 us -> 104 us  [run_layers(): pl.pallas_call(functools.partial(layers_kernel, n_tiles, n_layers), out_s...]
    another operation x1, loops' own time: 18.7 us -> 8.24 us  [body(): lax.while_loop(lambda c: c[0] * CAP < most, more, (jnp.int32(1), x_all, e...]
    pallas_call x1, Pallas kernels: 40.5 us -> 33.7 us  [run_mtp(): pl.pallas_call(functools.partial(mtp_kernel, n_proj, n_tiles), out_shape=...]
    another operation x1, loops' own time: 0.64 us -> 6.48 us  [body(): tile = lax.cond(stage == 0, tail_first, tail_last)]
where the time goes in v3:
time: 461 us; the launch traced here: 453 us
  Pallas kernels  429 us (93%)
  loops' own time  14.7 us (3%)
  local copies, waits for them, and re-layouts  7.57 us (2%)
    pallas_call x1, Pallas kernels, run_head(): pl.pallas_call(functools.partial(head_kernel, n_steps, tail, first), out_...  233 us
    pallas_call x2, Pallas kernels, run_layers(): pl.pallas_call(functools.partial(layers_kernel, n_tiles, n_layers), out_s...  104 us
    pallas_call x1, Pallas kernels, run_mtp(): pl.pallas_call(functools.partial(mtp_kernel, n_proj, n_tiles), out_shape=...  33.7 us
    pallas_call x1, Pallas kernels, run_trade(): pl.pallas_call(functools.partial(trade_kernel, n_data, n_local, n_seq), o...  24.4 us
    pallas_call x1, Pallas kernels, run_pack(): pl.pallas_call(functools.partial(pack_kernel, n_data), out_shape=jax.Shap...  13.1 us

profile of v3, /device:TPU:0, one launch (start us, length us, event | category | flops | bytes accessed | tf_op | source)
XLA Modules:
  0.0 452.9 jit_solution(15265636261742892091)
XLA Ops:
  0.6 0.7 reshape.247
  1.3 0.0 copy-start.7
  1.3 0.6 reshape.248.ids_ref
  1.9 8.9 %slots.1 = (s32[4,256]{1,0:T(4,128)}, s32[8,128]{1,0:T(8,128)}, s32[4,8,128]{2,1,0:T(8,128)S(1)}) custom-call(s32[8,128]{1,0:T(8,128)} %reshape.248.ids_ref), custom_call_target="tpu_custom_call" | custom-call | tf_op jit(solution)/shard_map/slots/pallas_call | solution.py:115
  10.9 0.0 copy-start.13
  10.9 13.1 %pack.1.packed_ref = bf16[4,160,2048]{2,1,0:T(8,128)(2,1)} custom-call(s32[4,256]{1,0:T(4,128)} %get-tuple-element.170.idx_ref.lane_ref, s32[4,256]{1,0:T(4,128)} %get-tuple-element.170.idx_ref.lane_ref, bf16[23136,2048]{1,0:T(8,128)(2,1)} %bitcast.10.table_ref), custom_call_target="tpu_custom_call" | custom-call | tf_op jit(solution)/shard_map/pack/pallas_call | solution.py:168
  24.0 0.0 copy-done.7
  24.0 24.4 %trade.1 = (bf16[576,2048]{1,0:T(8,128)(2,1)}, bf16[512,2048]{1,0:T(8,128)(2,1)}) custom-call(s32[8,128]{1,0:T(8,128)} %reshape.248.ids_ref, bf16[4,160,2048]{2,1,0:T(8,128)(2,1)} %pack.1.packed_ref), custom_call_target="tpu_custom_call" | custom-call | tf_op jit(solution)/shard_map/trade/pallas_call | solution.py:239
  48.5 0.0 copy-done.13
  48.5 1.2 slice.70
  49.7 8.2 %while.15 = (s32[]{:T(128)}, bf16[576,2048]{1,0:T(8,128)(2,1)}, bf16[512,2048]{1,0:T(8,128)(2,1)}, s32[]{:T(128)}, s32[4,8,128]{2,1,0:T(8,128)}, /*index=5*/bf16...) while((s32[]{:T(128)}, bf16[576,2048]{1,0:T(8,128)(2,1)}, ...), condition=%wide.wide.region_3.4_spmd, body=%wide.wide.region_0.3_spmd.sunk | while | flops 1376466304 | bytes 79386632 | solution.py:759
  57.9 0.0 copy-start.2
  57.9 51.9 %layers.4.x_ref = bf16[288,2048]{1,0:T(8,128)(2,1)} custom-call(bf16[576,2048]{1,0:T(8,128)(2,1)} %get-tuple-element.175.own_ref.got_ref, bf16[576,2048]{1,0:T(8,128)(2,1)} %get-tuple-element.175.own_ref.got_ref, bf16[1,2,2048,8192]{3,2,1,0:T(8,128)(2,1)} %w1_hbm.3, bf16[1,2,8192,2048]{3,2,1,0:T(8,128)(2,1)} %w2_hbm.3), custom_call_target="tpu_custom_call" | custom-call | flops 38654705664 | bytes 134217728 | tf_op jit(solution)/shard_map/layers/pallas_call | solution.py:467
  109.9 0.0 copy-done.2
  109.9 3.8 hand_on.1
  113.7 51.8 %layers.5.x_ref = bf16[288,2048]{1,0:T(8,128)(2,1)} custom-call(bf16[576,2048]{1,0:T(8,128)(2,1)} %get-tuple-element.175.own_ref.got_ref, bf16[288,2048]{1,0:T(8,128)(2,1)} %get-tuple-element.177.got_ref, bf16[1,2,2048,8192]{3,2,1,0:T(8,128)(2,1)} %w1_hbm.3, bf16[1,2,8192,2048]{3,2,1,0:T(8,128)(2,1)} %w2_hbm.3), custom_call_target="tpu_custom_call" | custom-call | flops 38654705664 | bytes 134217728 | tf_op jit(solution)/shard_map/layers/pallas_call | solution.py:467
  165.5 0.0 copy-start.8
  165.5 0.0 copy-start.3
  165.5 0.0 copy-start.9
  165.5 0.0 copy-start.10
  165.5 0.0 copy-start.11
  165.6 0.0 copy-start.12
  165.6 2.9 swap.1
  168.5 0.0 copy-done.8
  168.5 0.1 fusion.25
  168.6 0.0 copy-done.3
  168.6 0.0 copy-done.9
  168.6 0.0 copy-done.10
  168.6 0.0 copy-done.11
  168.6 0.0 copy-done.12
  168.6 275.8 %conditional.1 = (f32[8,128]{1,0:T(8,128)S(1)}) conditional(s32[]{:T(128)} %convert_element_type.29, (bf16[288,2048]{1,0:T(8,128)(2,1)S(1)}, bf16[1,2,2048,8192]{3,2,1,0:T(8,128)(2,1)}, bf16[1,2,8192,2048]{3,2,1,0:T(8,128)(2,1)}, bf16[2048]{0:T(1024)(128)(2,1)S(1)}, bf16[2048]{0:T(1024)(128)(2,1)S(1)}, /*index=5*/bf16[2048]{0:T(1024)(128)(2,1)S(1)}, ...), branch_computations={%region_4.5_spmd, %region_5.6_spmd} | conditional | flops 242497880064 | bytes 600866816 | solution.py:775
  174.8 0.6 broadcast_in_dim.69.gf_ref
  175.4 0.6 broadcast_in_dim.70.gh_ref
  176.0 0.6 broadcast_in_dim.71.ge_ref
  176.6 0.6 broadcast_in_dim.72.gm_ref
  177.2 33.7 %mtp.3.x_ref = bf16[576,2048]{1,0:T(8,128)(2,1)} custom-call(bf16[288,2048]{1,0:T(8,128)(2,1)S(1)} %get-tuple-element.145.h_ref, bf16[512,2048]{1,0:T(8,128)(2,1)S(1)} %get-tuple-element.146.e_ref, bf16[1,2048]{1,0:T(2,128)(2,1)} %broadcast_in_dim.69.gf_ref, bf16[1,2048]{1,0:T(2,128)(2,1)} %broadcast_in_dim.70.gh_ref, ...), custom_call_target="tpu_custom_call" | custom-call | flops 24159191040 | bytes 83886080 | tf_op jit(solution)/shard_map/cond/branch_1_fun/mtp/pallas_call | solution.py:572
  210.9 233.2 %head.3 = f32[8,128]{1,0:T(8,128)S(1)} custom-call(bf16[576,2048]{1,0:T(8,128)(2,1)} %mtp.3.x_ref, s32[8,128]{1,0:T(8,128)S(1)} %get-tuple-element.154.tgt_ref, bf16[2048,92544]{1,0:T(8,128)(2,1)} %get-tuple-element.155.w_ref), custom_call_target="tpu_custom_call" | custom-call | flops 218338689024 | bytes 379060224 | tf_op jit(solution)/shard_map/cond/branch_1_fun/head/pallas_call | solution.py:682
  444.4 5.4 %finish.1 = (f32[8,128]{1,0:T(8,128)}, f32[8,128]{1,0:T(8,128)}) custom-call(f32[8,128]{1,0:T(8,128)S(1)} %get-tuple-element.353.x_ref), custom_call_target="tpu_custom_call" | custom-call | tf_op jit(solution)/shard_map/finish/pallas_call | solution.py:341
  449.9 1.3 fusion.24
  451.2 1.2 slice.73
  (3 shorter events, 0.0 us)
Async XLA Ops:
  1.3 22.7 %copy-start.7 = (s32[4,130]{1,0:T(4,128)}, s32[4,130]{1,0:T(4,128)S(1)}, u32[]{:S(2)}) copy-start(s32[4,130]{1,0:T(4,128)S(1)} %reshape.247) | copy-start | bytes 6244
  10.9 37.6 %copy-start.13 = (s32[4,8,128]{2,1,0:T(8,128)}, s32[4,8,128]{2,1,0:T(8,128)S(1)}, u32[]{:S(2)}) copy-start(s32[4,8,128]{2,1,0:T(8,128)S(1)} %get-tuple-element.318) | copy-start | bytes 49156
  57.9 51.9 %copy-start.2 = (bf16[512,2048]{1,0:T(8,128)(2,1)S(1)}, bf16[512,2048]{1,0:T(8,128)(2,1)}, u32[]{:S(2)}) copy-start(bf16[512,2048]{1,0:T(8,128)(2,1)} %get-tuple-element.176.e_ref) | copy-start | bytes 6291460
  165.5 3.0 copy-start.8
  165.5 3.0 copy-start.3
  165.5 3.0 copy-start.9
  165.5 3.0 copy-start.10
  165.5 3.0 copy-start.11
  165.6 3.0 copy-start.12

commit v4 on v3

--- a/solution.py
+++ b/solution.py
@@ -22,7 +22,7 @@
 HEAD_HALF = 1024
 HEAD_PARTS = 4
 CAP = 160
-SLOTS = 3
+SLOTS = 4
 BLOCK = 8
 
 
@@ -358,7 +358,13 @@
     return pltpu.make_async_copy(src, ring.at[slot], sems.at[slot])
 
 
-def ffn_steps(j, n_tiles, n_s, w1_slot, w2_slot, ring1, ring2, raw, hid, acc, finish):
+def ffn_steps(j, n_tiles, n_s, ready1, ready2, ring1, ring2, first, raw, hid, acc, finish):
+    def slot1(t):
+        return ring1[lax.rem(first[0] + t, SLOTS)]
+
+    def slot2(t):
+        return ring2[lax.rem(first[1] + t, SLOTS)]
+
     def activate():
         for r in range(0, raw.shape[0], GROUP):
             for c in range(0, raw.shape[1], 2 * LANES):
@@ -367,26 +373,55 @@
 
     @pl.when(j == 0)
     def _():
-        raw[...] = dot32(n_s[...], ring1[w1_slot])
-
-    @pl.when((j > 0) & (j < n_tiles))
-    def _():
+        ready1(0)
+        raw[...] = dot32(n_s[...], slot1(0))
+
+    @pl.when(j == 0)
+    def _():
+        ready1(1)
+        ready2(0)
         activate()
-        raw[...] = dot32(n_s[...], ring1[w1_slot])
-        acc[...] += dot32(hid[...], ring2[w2_slot])
-
-    @pl.when(j == n_tiles)
-    def _():
+        raw[...] = dot32(n_s[...], slot1(1))
+        acc[...] = dot32(hid[...], slot2(0))
+
+    @pl.when((j > 0) & (2 * j < n_tiles))
+    def _():
+        ready1(2 * j)
+        ready1(2 * j + 1)
+        ready2(2 * j - 1)
+        ready2(2 * j)
         activate()
-        acc[...] += dot32(hid[...], ring2[w2_slot])
+        raw[...] = dot32(n_s[...], slot1(2 * j))
+        acc[...] += dot32(hid[...], slot2(2 * j - 1))
+        activate()
+        raw[...] = dot32(n_s[...], slot1(2 * j + 1))
+        acc[...] += dot32(hid[...], slot2(2 * j))
+
+    @pl.when(2 * j == n_tiles)
+    def _():
+        ready2(n_tiles - 1)
+        activate()
+        acc[...] += dot32(hid[...], slot2(n_tiles - 1))
         finish()
 
 
-def layers_kernel(n_tiles, n_layers, own_ref, got_ref, w1_hbm, w2_hbm, o_ref, x_s, n_s, raw, hid, acc, ring1, ring2, sem1, sem2):
+def layers_kernel(last_only, *refs):
+    stage = lax.axis_index("pp")
+    if last_only:
+        @pl.when(stage != 0)
+        def _():
+            layers_body(*refs)
+    else:
+        layers_body(*refs)
+
+
+def layers_body(own_ref, got_ref, w1_hbm, w2_hbm, o_ref, x_s, n_s, raw, hid, acc, ring1, ring2, sem1, sem2):
     layer, j = pl.program_id(0), pl.program_id(1)
     stage = lax.axis_index("pp")
+    n_layers = w1_hbm.shape[1]
+    n_tiles = w1_hbm.shape[3] // FFN_TILE
     total = n_layers * n_tiles
-    up, down = layer * n_tiles + j, layer * n_tiles + j - 1
+    first = layer * n_tiles
 
     def copy1(i):
         col = pl.multiple_of(lax.rem(i, n_tiles) * FFN_TILE, FFN_TILE)
@@ -413,29 +448,44 @@
     @pl.when(j == 0)
     def _():
         norm_rows(n_s, x_s)
-        acc[...] = jnp.zeros_like(acc)
 
     @pl.when(start)
     def _():
         copy1(1).start()
         copy2(0).start()
-        copy2(1).start()
-
-    @pl.when(j < n_tiles)
-    def _():
-        copy1(up).wait()
-
-        @pl.when(up + SLOTS - 1 < total)
+
+    def feed(copy, i):
+        @pl.when((2 * j < n_tiles) & (i < total))
         def _():
-            copy1(up + SLOTS - 1).start()
-
-    @pl.when(j > 0)
-    def _():
-        copy2(down).wait()
-
-        @pl.when(down + SLOTS - 1 < total)
-        def _():
-            copy2(down + SLOTS - 1).start()
+            copy(i).start()
+
+    def ready1(t):
+        copy1(first + t).wait()
+
+    def ready2(t):
+        copy2(first + t).wait()
+
+    @pl.when(jnp.logical_not(start))
+    def _():
+        feed(copy1, first + 2 * j + 2)
+        feed(copy2, first + 2 * j + 1)
+        feed(copy1, first + 2 * j + 3)
+        feed(copy2, first + 2 * j + 2)
+
+    @pl.when(start)
+    def _():
+        copy1(0).wait()
+        for i in (2, 3):
+            copy1(i).start()
+            copy2(i - 1).start()
+
+    def ready1_once(t):
+        if isinstance(t, int) and t == 0:
+            @pl.when(layer > 0)
+            def _():
+                ready1(0)
+        else:
+            ready1(t)
 
     def finish():
         for r in range(0, x_s.shape[0], GROUP):
@@ -444,9 +494,7 @@
             x_s[rs, :] = out
             o_ref[rs, :] = out
 
-    ffn_steps(
-        j, n_tiles, n_s, lax.rem(up, SLOTS), lax.rem(jnp.maximum(down, 0), SLOTS), ring1, ring2, raw, hid, acc, finish
-    )
+    ffn_steps(j, n_tiles, n_s, ready1_once, ready2, ring1, ring2, (first, first), raw, hid, acc, finish)
 
 
 def ring_scratch(width):
@@ -458,16 +506,16 @@
     ]
 
 
-def run_layers(own, own_block, got, rows, w_one, w_two):
+def run_layers(own, own_block, got, rows, w_one, w_two, last_only=False):
     width = own.shape[1]
     _, n_layers, _, ffn = w_one.shape
     n_tiles = ffn // FFN_TILE
     whole = pl.BlockSpec((rows, width), lambda l, j: (0, 0))
     hbm = pl.BlockSpec(memory_space=pl.ANY)
     return pl.pallas_call(
-        functools.partial(layers_kernel, n_tiles, n_layers),
+        functools.partial(layers_kernel, last_only),
         out_shape=jax.ShapeDtypeStruct((rows, width), BF16),
-        grid=(n_layers, n_tiles + 1),
+        grid=(n_layers, n_tiles // 2 + 1),
         in_specs=[pl.BlockSpec((rows, width), lambda l, j: (own_block, 0)), whole, hbm, hbm],
         out_specs=whole,
         scratch_shapes=[
@@ -486,97 +534,124 @@
 
 
 def mtp_kernel(
-    n_proj, n_tiles, h_ref, e_ref, gf_ref, gh_ref, ge_ref, gm_ref, wp_hbm, w1_hbm, w2_hbm, o_ref,
+    n_proj, n_tiles, own_h, own_e, got_h, got_e, gain_ref, wp_hbm, w1_hbm, w2_hbm, o_ref,
     cat_s, z_s, n_s, raw, hid, acc, ring1, ring2, sem1, sem2,
 ):
     step = pl.program_id(0)
-    rows, width = h_ref.shape
-    j = step - n_proj
-    total2 = n_proj + n_tiles
-    second = jnp.where(step < n_proj, step, step - 1)
+    stage = lax.axis_index("pp")
+    rows, width = own_h.shape
+    rows_b = got_h.shape[0]
+    proj_steps = n_proj // 2
+    j = step - proj_steps
+    gf_ref, gh_ref, ge_ref, gm_ref = (gain_ref.at[k:k + 1, :] for k in range(4))
 
     def copy1(i):
         col = pl.multiple_of(i * FFN_TILE, FFN_TILE)
         return ring_copy(w1_hbm.at[:, pl.ds(col, FFN_TILE)], ring1, sem1, i)
 
-    def copy2(src, i, tile):
-        row = pl.multiple_of(tile * FFN_TILE, FFN_TILE)
-        return ring_copy(src.at[pl.ds(row, FFN_TILE), :], ring2, sem2, i)
-
-    def feed2(i):
-        @pl.when(i < n_proj)
+    def copy2(i):
+        row = pl.multiple_of((i - n_proj) * FFN_TILE, FFN_TILE)
+        return ring_copy(w2_hbm.at[pl.ds(row, FFN_TILE), :], ring2, sem2, i)
+
+    def copyp(i):
+        return ring_copy(wp_hbm.at[pl.ds(i * FFN_TILE, FFN_TILE), :], ring2, sem2, i)
+
+    @pl.when(step == 0)
+    def _():
+        copyp(0).start()
+        copyp(1).start()
+
+    @pl.when((step == 0) & (stage == 0))
+    def _():
+        z_s[...] = own_h[...]
+        n_s[...] = own_e[...]
+
+    @pl.when((step == 0) & (stage != 0))
+    def _():
+        z_s[:rows_b, :] = got_h[...]
+        n_s[:rows_b, :] = got_e[...]
+        if rows_b < rows:
+            z_s[rows_b:, :] = jnp.zeros((rows - rows_b, width), BF16)
+            n_s[rows_b:, :] = jnp.zeros((rows - rows_b, width), BF16)
+
+    @pl.when(step == 0)
+    def _():
+        norm_rows(cat_s.at[:, pl.ds(0, width)], z_s, gh_ref)
+        norm_rows(cat_s.at[:, pl.ds(width, width)], n_s, ge_ref)
+        norm_rows(o_ref, z_s, gf_ref)
+        acc[...] = jnp.zeros_like(acc)
+        copyp(2).start()
+        copyp(3).start()
+
+    for p in range(proj_steps):
+        @pl.when(step == p)
         def _():
-            copy2(wp_hbm, i, i).start()
-
-        @pl.when((i >= n_proj) & (i < total2))
-        def _():
-            copy2(w2_hbm, i, i - n_proj).start()
-
-    @pl.when(step == 0)
-    def _():
-        copy2(wp_hbm, 0, 0).start()
-        norm_rows(cat_s.at[:, pl.ds(0, width)], h_ref, gh_ref)
-        norm_rows(cat_s.at[:, pl.ds(width, width)], e_ref, ge_ref)
-        norm_rows(o_ref, h_ref, gf_ref)
-        acc[...] = jnp.zeros_like(acc)
-        copy2(wp_hbm, 1, 1).start()
-
-    @pl.when(step == n_proj - 2)
-    def _():
-        copy1(0).start()
-        copy1(1).start()
-
-    @pl.when(j != 0)
-    def _():
-        copy2(wp_hbm, second, 0).wait()
-        feed2(second + SLOTS - 1)
-
-    @pl.when((j >= 0) & (j < n_tiles))
-    def _():
-        copy1(j).wait()
-
-        @pl.when(j + SLOTS - 1 < n_tiles)
-        def _():
-            copy1(j + SLOTS - 1).start()
-
-    @pl.when(step < n_proj)
-    def _():
-        at = pl.multiple_of(step * FFN_TILE, FFN_TILE)
-        acc[...] += dot32(cat_s[:, pl.ds(at, FFN_TILE)], ring2[lax.rem(second, SLOTS)])
-
-    @pl.when(step == n_proj - 1)
+            for t in (2 * p, 2 * p + 1):
+                copyp(t).wait()
+            if p == proj_steps - 1:
+                copy1(0).start()
+                copy1(1).start()
+                copy2(n_proj).start()
+
+    @pl.when(step < proj_steps)
+    def _():
+        for half in range(2):
+            at = pl.multiple_of((2 * step + half) * FFN_TILE, FFN_TILE)
+            acc[...] += dot32(cat_s[:, pl.ds(at, FFN_TILE)], ring2[lax.rem(2 * step + half, SLOTS)])
+
+    @pl.when(step == proj_steps - 1)
     def _():
         for r in range(0, rows, GROUP):
             z_s[r:r + GROUP, :] = acc[r:r + GROUP, :].astype(BF16)
         norm_rows(n_s, z_s, gm_ref)
-        acc[...] = jnp.zeros_like(acc)
+
+    def feed(copy, i, end):
+        @pl.when((j >= 0) & (2 * j < n_tiles) & (i < end))
+        def _():
+            copy(i).start()
+
+    feed(copy1, 2 * j + 2, n_tiles)
+    feed(copy2, n_proj + 2 * j + 1, n_proj + n_tiles)
+    feed(copy1, 2 * j + 3, n_tiles)
+    feed(copy2, n_proj + 2 * j + 2, n_proj + n_tiles)
+
+    def ready1(t):
+        copy1(t).wait()
+
+    def ready2(t):
+        copy2(n_proj + t).wait()
 
     def finish():
         for r in range(0, rows, GROUP):
             rs = slice(r, r + GROUP)
             z_s[rs, :] = (z_s[rs, :].astype(F32) + acc[rs, :]).astype(BF16)
+
+    ffn_steps(j, n_tiles, n_s, ready1, ready2, ring1, ring2, (0, n_proj), raw, hid, acc, finish)
+
+    @pl.when((2 * j == n_tiles) & (stage == 0))
+    def _():
         norm_rows(o_ref, z_s, gf_ref, rows)
 
-    ffn_steps(
-        j, n_tiles, n_s, lax.rem(jnp.maximum(j, 0), SLOTS), lax.rem(second, SLOTS), ring1, ring2, raw, hid, acc, finish
-    )
-
-
-def run_mtp(h_last, e_rows, rows, gain_f, gain_h, gain_e, gain_m, w_proj, u_one, u_two):
-    width = h_last.shape[1]
+    @pl.when((2 * j == n_tiles) & (stage != 0))
+    def _():
+        norm_rows(o_ref, z_s.at[pl.ds(0, rows_b), :], gf_ref, rows_b)
+
+
+def run_mtp(own_h, own_e, got_h, got_e, gains, w_proj, u_one, u_two):
+    rows, width = own_h.shape
+    rows_b = got_h.shape[0]
     ffn = u_one.shape[1]
     n_tiles = ffn // FFN_TILE
     n_proj = w_proj.shape[0] // FFN_TILE
+    assert n_proj == SLOTS
     whole = pl.BlockSpec((rows, width), lambda s: (0, 0))
-    gain = pl.BlockSpec((1, width), lambda s: (0, 0))
+    other = pl.BlockSpec((rows_b, width), lambda s: (0, 0))
+    hbm = pl.BlockSpec(memory_space=pl.ANY)
     return pl.pallas_call(
         functools.partial(mtp_kernel, n_proj, n_tiles),
         out_shape=jax.ShapeDtypeStruct((2 * rows, width), BF16),
-        grid=(n_proj + n_tiles + 1,),
-        in_specs=[
-            whole, whole, gain, gain, gain, gain,
-            pl.BlockSpec(memory_space=pl.ANY), pl.BlockSpec(memory_space=pl.ANY), pl.BlockSpec(memory_space=pl.ANY),
-        ],
+        grid=(n_proj // 2 + n_tiles // 2 + 1,),
+        in_specs=[whole, whole, other, other, pl.BlockSpec(gains.shape, lambda s: (0, 0)), hbm, hbm, hbm],
         out_specs=pl.BlockSpec((2 * rows, width), lambda s: (0, 0)),
         scratch_shapes=[
             pltpu.VMEM((rows, 2 * width), BF16),
@@ -591,11 +666,10 @@
             flops=4 * rows * width * (ffn + width), bytes_accessed=4 * width * (ffn + width), transcendentals=0
         ),
         name="mtp",
-    )(h_last, e_rows, gain_f[None], gain_h[None], gain_e[None], gain_m[None], w_proj, u_one, u_two)
-
-
-def head_stats(buf, n_cols, base, tgt_ref, m_ref, s_ref, p_ref):
-    rows = buf.shape[0]
+    )(own_h, own_e, got_h, got_e, gains, w_proj, u_one, u_two)
+
+
+def head_stats(rows, buf, n_cols, base, tgt_ref, m_ref, s_ref, p_ref):
     lane = lax.broadcasted_iota(jnp.int32, (GROUP, LANES), 1)
     for r in range(0, rows, GROUP):
         rs = slice(r, r + GROUP)
@@ -616,51 +690,59 @@
         p_ref[rs, :] = pick
 
 
-def head_kernel(n_steps, tail, first, x_ref, tgt_ref, w_ref, o_ref, buf_a, buf_b, t_ref, m_ref, s_ref, p_ref):
+def head_kernel(n_steps, tail, parts, x_ref, tgt_ref, w_ref, o_ref, buf_a, buf_b, t_ref, m_ref, s_ref, p_ref):
+    stage = lax.axis_index("pp")
+    for s, (first, count) in enumerate(parts):
+        @pl.when(stage == s)
+        def _():
+            head_body(n_steps, tail, first, count, x_ref, tgt_ref, w_ref, o_ref, buf_a, buf_b, t_ref, m_ref, s_ref, p_ref)
+
+
+def head_body(n_steps, tail, first, count, x_ref, tgt_ref, w_ref, o_ref, buf_a, buf_b, t_ref, m_ref, s_ref, p_ref):
     i = pl.program_id(0)
     half = buf_a.shape[1]
-    rows = x_ref.shape[0] // 2
+    rows = 2 * count
     n_seq = tgt_ref.shape[0] // 2
+    bufs = (buf_a, buf_b)
     state = (t_ref, m_ref, s_ref, p_ref)
     row = lax.broadcasted_iota(I32, (GROUP, LANES), 0)
     lane = lax.broadcasted_iota(I32, (GROUP, LANES), 1)
 
     @pl.when(i == 0)
     def _():
-        buf_b[...] = jnp.full_like(buf_b, -3e38)
         m_ref[...] = jnp.full_like(m_ref, -3e38)
         s_ref[...] = jnp.zeros_like(s_ref)
         p_ref[...] = jnp.zeros_like(p_ref)
         for part in range(2):
-            for r in range(0, rows, GROUP):
+            for r in range(0, count, GROUP):
                 want = jnp.zeros((GROUP, LANES), F32)
                 for q in range(n_seq):
                     line = tgt_ref[part * n_seq + q:part * n_seq + q + 1, :].astype(F32)
                     want = want + jnp.where(q * LANES + lane == first + r + row, jnp.broadcast_to(line, want.shape), 0.0)
                 want = jnp.sum(want, axis=1, keepdims=True)
-                at = part * rows + r
+                at = part * count + r
                 t_ref[at:at + GROUP, :] = jnp.broadcast_to(want, (GROUP, LANES)).astype(I32)
-
-    @pl.when(i < n_steps - 1)
-    def _():
-        bufs = (buf_a, buf_b)
+        base = (n_steps - 1) * HEAD_PARTS * half
+        for k, done in enumerate(range(0, tail, half)):
+            cols = min(half, tail - done)
+            bufs[k % 2][:rows, :cols] = dot32(x_ref[:rows, :], w_ref[:, done:done + cols])
+            head_stats(rows, bufs[k % 2], cols, base + done, *state)
+        buf_b[...] = jnp.full_like(buf_b, -3e38)
+
+    @pl.when(i > 0)
+    def _():
+        base = (i - 1) * HEAD_PARTS * half
         for q in range(HEAD_PARTS):
-            bufs[q % 2][...] = dot32(x_ref[...], w_ref[:, q * half:(q + 1) * half])
-            head_stats(bufs[(q + 1) % 2], half, (HEAD_PARTS * i + q - 1) * half, *state)
+            bufs[q % 2][:rows, :] = dot32(x_ref[:rows, :], w_ref[:, q * half:(q + 1) * half])
+            head_stats(rows, bufs[(q + 1) % 2], half, base + (q - 1) * half, *state)
 
     @pl.when(i == n_steps - 1)
     def _():
-        head_stats(buf_b, half, (HEAD_PARTS * i - 1) * half, *state)
-        done = 0
-        while done < tail:
-            cols = min(half, tail - done)
-            buf_a[:, :cols] = dot32(x_ref[...], w_ref[:, done:done + cols])
-            head_stats(buf_a, cols, HEAD_PARTS * i * half + done, *state)
-            done += cols
+        head_stats(rows, buf_b, half, (i * HEAD_PARTS - 1) * half, *state)
         for part in range(2):
             lines = [jnp.zeros((1, LANES), F32) for _ in range(n_seq)]
-            for r in range(0, rows, GROUP):
-                rs = slice(part * rows + r, part * rows + r + GROUP)
+            for r in range(0, count, GROUP):
+                rs = slice(part * count + r, part * count + r + GROUP)
                 top = jnp.max(m_ref[rs, :], axis=1, keepdims=True)
                 total = jnp.sum(s_ref[rs, :] * jnp.exp(m_ref[rs, :] - top), axis=1, keepdims=True)
                 picked = jnp.sum(p_ref[rs, :], axis=1, keepdims=True)
@@ -672,7 +754,7 @@
             o_ref[part * n_seq:(part + 1) * n_seq, :] = jnp.concatenate(lines, axis=0)
 
 
-def run_head(x_val, tgt_tile, first, w_out):
+def run_head(x_val, tgt_tile, parts, w_out):
     rows, width = x_val.shape
     vocab = w_out.shape[1]
     tile = HEAD_PARTS * HEAD_HALF
@@ -680,13 +762,13 @@
     tail = vocab - (n_steps - 1) * tile
     small = pl.BlockSpec(tgt_tile.shape, lambda i: (0, 0))
     return pl.pallas_call(
-        functools.partial(head_kernel, n_steps, tail, first),
+        functools.partial(head_kernel, n_steps, tail, parts),
         out_shape=jax.ShapeDtypeStruct(tgt_tile.shape, F32),
         grid=(n_steps,),
         in_specs=[
             pl.BlockSpec((rows, width), lambda i: (0, 0)),
             small,
-            pl.BlockSpec((width, tile), lambda i: (0, i)),
+            pl.BlockSpec((width, tile), lambda i: (0, jnp.where(i == 0, n_steps - 1, i - 1))),
         ],
         out_specs=small,
         scratch_shapes=[pltpu.VMEM((rows, HEAD_HALF), F32)] * 2
@@ -728,7 +810,6 @@
         return dot32(pick, jnp.concatenate(got, axis=0)).astype(BF16)
 
     def body(tok_ids, emb_s, w_one, w_two, gain_f, gain_h, gain_e, gain_m, w_proj, u_one, u_two, w_out):
-        stage = lax.axis_index("pp")
         n_micro, batch_dev, seq_plus = tok_ids.shape
         seq_len = seq_plus - 2
         n_seq = n_micro * batch_dev
@@ -762,17 +843,10 @@
         moved, e_last = run_hand_on(x_mid, e_all)
         swapped = run_swap(run_layers(x_all, 1, moved, rows_a, w_one, w_two))
 
-        def tail(h_last, e_rows, first, rows):
-            normed = run_mtp(h_last, e_rows, rows, gain_f, gain_h, gain_e, gain_m, w_proj, u_one, u_two)
-            return run_head(normed, tgt_tile, first, w_out)
-
-        def tail_first():
-            return tail(swapped, e_all, 0, rows_a)
-
-        def tail_last():
-            return tail(run_layers(swapped, 0, swapped, rows_b, w_one, w_two), e_last, rows_a, rows_b)
-
-        tile = lax.cond(stage == 0, tail_first, tail_last)
+        h_last = run_layers(swapped, 0, swapped, rows_b, w_one, w_two, last_only=True)
+        gains = jnp.stack([gain_f, gain_h, gain_e, gain_m] * 2).astype(F32)
+        normed = run_mtp(swapped, e_all, h_last, e_last, gains, w_proj, u_one, u_two)
+        tile = run_head(normed, tgt_tile, ((0, rows_a), (rows_a, rows_b)), w_out)
         nll, total = run_finish(tile, n_data, n_stages, 1.0 / (n_tok * n_data))
         shape = (n_micro, batch_dev, seq_len)
         return total[0, 0], nll[:n_seq].reshape(shape), nll[n_seq:].reshape(shape)

time: 461 us -> 487 us (1.056)
  Pallas kernels: 429 us -> 465 us
  loops' own time: 14.7 us -> 7.16 us
    pallas_call x3 -> x4, Pallas kernels: 337 us -> 361 us  [the longest x1 249 us: run_head(): pl.pallas_call(functools.partial(head_kernel, n_steps, tail, parts), out_...]
    pallas_call x1, Pallas kernels: 33.7 us -> 43.5 us  [run_mtp(): pl.pallas_call(functools.partial(mtp_kernel, n_proj, n_tiles), out_shape=...]
    another operation x1 -> x0, loops' own time: 6.48 us -> none  [body(): tile = lax.cond(stage == 0, tail_first, tail_last)]
where the time goes in v4:
time: 487 us; the launch traced here: 479 us
  Pallas kernels  465 us (95%)
  loops' own time  7.16 us (1%)
  local copies, waits for them, and re-layouts  5.3 us (1%)
    pallas_call x1, Pallas kernels, run_head(): pl.pallas_call(functools.partial(head_kernel, n_steps, tail, parts), out_...  249 us
    pallas_call x3, Pallas kernels, run_layers(): pl.pallas_call(functools.partial(layers_kernel, last_only), out_shape=jax...  112 us
    pallas_call x1, Pallas kernels, run_mtp(): pl.pallas_call(functools.partial(mtp_kernel, n_proj, n_tiles), out_shape=...  43.5 us
    pallas_call x1, Pallas kernels, run_trade(): pl.pallas_call(functools.partial(trade_kernel, n_data, n_local, n_seq), o...  26.2 us
    pallas_call x1, Pallas kernels, run_pack(): pl.pallas_call(functools.partial(pack_kernel, n_data), out_shape=jax.Shap...  12 us

profile of v4, /device:TPU:0, one launch (start us, length us, event | category | flops | bytes accessed | tf_op | source)
XLA Modules:
  0.0 479.4 jit_solution(367573564020891488)
XLA Ops:
  0.6 0.7 reshape.247
  1.3 0.0 copy-start.5
  1.3 0.6 reshape.248.ids_ref
  1.9 8.9 %slots.1 = (s32[4,256]{1,0:T(4,128)}, s32[8,128]{1,0:T(8,128)}, s32[4,8,128]{2,1,0:T(8,128)S(1)}) custom-call(s32[8,128]{1,0:T(8,128)} %reshape.248.ids_ref), custom_call_target="tpu_custom_call" | custom-call | tf_op jit(solution)/shard_map/slots/pallas_call | solution.py:115
  10.9 0.0 copy-start.7
  10.9 12.0 %pack.1.packed_ref = bf16[4,160,2048]{2,1,0:T(8,128)(2,1)} custom-call(s32[4,256]{1,0:T(4,128)} %get-tuple-element.95.idx_ref.lane_ref, s32[4,256]{1,0:T(4,128)} %get-tuple-element.95.idx_ref.lane_ref, bf16[23136,2048]{1,0:T(8,128)(2,1)} %bitcast.10.table_ref), custom_call_target="tpu_custom_call" | custom-call | tf_op jit(solution)/shard_map/pack/pallas_call | solution.py:168
  22.9 0.0 copy-done.5
  22.9 26.2 %trade.1 = (bf16[576,2048]{1,0:T(8,128)(2,1)}, bf16[512,2048]{1,0:T(8,128)(2,1)}) custom-call(s32[8,128]{1,0:T(8,128)} %reshape.248.ids_ref, bf16[4,160,2048]{2,1,0:T(8,128)(2,1)} %pack.1.packed_ref), custom_call_target="tpu_custom_call" | custom-call | tf_op jit(solution)/shard_map/trade/pallas_call | solution.py:239
  49.1 0.0 copy-done.7
  49.2 1.2 slice.70
  50.4 7.2 %while.15 = (s32[]{:T(128)}, bf16[576,2048]{1,0:T(8,128)(2,1)}, bf16[512,2048]{1,0:T(8,128)(2,1)}, s32[]{:T(128)}, s32[4,8,128]{2,1,0:T(8,128)}, /*index=5*/bf16...) while((s32[]{:T(128)}, bf16[576,2048]{1,0:T(8,128)(2,1)}, ...), condition=%wide.wide.region_3.4_spmd, body=%wide.wide.region_0.3_spmd.sunk | while | flops 1376466304 | bytes 79386632 | solution.py:840
  57.5 0.0 copy-start.2
  57.5 54.7 %layers.3.x_ref = bf16[288,2048]{1,0:T(8,128)(2,1)} custom-call(bf16[576,2048]{1,0:T(8,128)(2,1)} %get-tuple-element.100.refs_0_.refs_1_, bf16[576,2048]{1,0:T(8,128)(2,1)} %get-tuple-element.100.refs_0_.refs_1_, bf16[1,2,2048,8192]{3,2,1,0:T(8,128)(2,1)} %refs_2_.5, bf16[1,2,8192,2048]{3,2,1,0:T(8,128)(2,1)} %refs_3_.5), custom_call_target="tpu_custom_call" | custom-call | flops 38654705664 | bytes 134217728 | tf_op jit(solution)/shard_map/layers/pallas_call | solution.py:515
  112.3 0.0 copy-done.2
  112.3 3.8 hand_on.1
  116.1 55.0 %layers.4.x_ref = bf16[288,2048]{1,0:T(8,128)(2,1)} custom-call(bf16[576,2048]{1,0:T(8,128)(2,1)} %get-tuple-element.100.refs_0_.refs_1_, bf16[288,2048]{1,0:T(8,128)(2,1)} %get-tuple-element.102.refs_1_, bf16[1,2,2048,8192]{3,2,1,0:T(8,128)(2,1)} %refs_2_.5, bf16[1,2,8192,2048]{3,2,1,0:T(8,128)(2,1)} %refs_3_.5), custom_call_target="tpu_custom_call" | custom-call | flops 38654705664 | bytes 134217728 | tf_op jit(solution)/shard_map/layers/pallas_call | solution.py:515
  171.1 2.8 swap.1.refs_0_.refs_1_.own_h
  174.0 0.0 copy-start.8
  174.0 0.0 copy-start.9
  174.0 0.0 copy-start.10
  174.0 0.0 copy-start.11
  174.0 2.7 layers.5.got_h
  176.7 0.0 copy-done.8
  176.8 0.0 copy-done.9
  176.8 0.0 copy-done.10
  176.8 0.0 copy-done.11
  176.8 0.1 stack.23
  176.9 0.6 convert_element_type.29.gain_ref
  177.6 0.0 copy-start.6
  177.6 43.5 %mtp.1.x_ref = bf16[576,2048]{1,0:T(8,128)(2,1)} custom-call(bf16[288,2048]{1,0:T(8,128)(2,1)} %swap.1.refs_0_.refs_1_.own_h, bf16[512,2048]{1,0:T(8,128)(2,1)S(1)} %copy-done.2, bf16[224,2048]{1,0:T(8,128)(2,1)} %layers.5.got_h, bf16[224,2048]{1,0:T(8,128)(2,1)} %get-tuple-element.103.got_e, f32[8,2048]{1,0:T(8,128)} %convert_element_type.29.gain_ref, ...), custom_call_target="tpu_custom_call" | custom-call | flops 24159191040 | bytes 83886080 | tf_op jit(solution)/shard_map/mtp/pallas_call | solution.py:650
  221.1 0.0 copy-done.6
  221.1 0.1 fusion.25
  221.2 0.6 pad_add_fusion.1.tgt_ref
  221.8 248.8 %head.1.x_ref = f32[8,128]{1,0:T(8,128)} custom-call(bf16[576,2048]{1,0:T(8,128)(2,1)} %mtp.1.x_ref, s32[8,128]{1,0:T(8,128)} %pad_add_fusion.1.tgt_ref, bf16[2048,92544]{1,0:T(8,128)(2,1)} %w_ref.1), custom_call_target="tpu_custom_call" | custom-call | flops 218338689024 | bytes 379060224 | tf_op jit(solution)/shard_map/head/pallas_call | solution.py:764
  470.6 6.1 %finish.1 = (f32[8,128]{1,0:T(8,128)}, f32[8,128]{1,0:T(8,128)}) custom-call(f32[8,128]{1,0:T(8,128)} %head.1.x_ref), custom_call_target="tpu_custom_call" | custom-call | tf_op jit(solution)/shard_map/finish/pallas_call | solution.py:341
  476.7 1.3 fusion.24
  478.0 1.2 slice.73
  (6 shorter events, 0.0 us)
Async XLA Ops:
  1.3 21.6 %copy-start.5 = (s32[4,130]{1,0:T(4,128)}, s32[4,130]{1,0:T(4,128)S(1)}, u32[]{:S(2)}) copy-start(s32[4,130]{1,0:T(4,128)S(1)} %reshape.247) | copy-start | bytes 6244
  10.9 38.3 %copy-start.7 = (s32[4,8,128]{2,1,0:T(8,128)}, s32[4,8,128]{2,1,0:T(8,128)S(1)}, u32[]{:S(2)}) copy-start(s32[4,8,128]{2,1,0:T(8,128)S(1)} %get-tuple-element.243) | copy-start | bytes 49156
  57.5 54.8 %copy-start.2 = (bf16[512,2048]{1,0:T(8,128)(2,1)S(1)}, bf16[512,2048]{1,0:T(8,128)(2,1)}, u32[]{:S(2)}) copy-start(bf16[512,2048]{1,0:T(8,128)(2,1)} %get-tuple-element.101.e_ref.own_e) | copy-start | bytes 6291460
  174.0 2.8 copy-start.8
  174.0 2.8 copy-start.9
  174.0 2.8 copy-start.10
  174.0 2.8 copy-start.11
  177.6 43.5 %copy-start.6 = (s32[4,130]{1,0:T(4,128)S(1)}, s32[4,130]{1,0:T(4,128)}, u32[]{:S(2)}) copy-start(s32[4,130]{1,0:T(4,128)} %copy-done.5) | copy-start | bytes 6244
